TPU v7x, 8 devices: a whole 2x2x1 slice. The times are simulated.
8 devices in a mesh: frag: 1 (over z), dev: 8 (over y, x, core).
Axes of the slice: x: 2, y: 2, z: 1, core: 2. Of those that a mesh axis runs over, the one named last changes fastest.
Arguments:
- ao_ints: bfloat16 [112, 112, 112, 112], P(('frag', 'dev'))
- c_occ: bfloat16 [112, 16], P('frag')
- c_vir: bfloat16 [112, 88], P('frag')
Outputs:
- output 1: float32 [88, 88, 256], P('frag', None, 'dev')
- output 2: float32 [16, 88, 1408], P('frag', None, 'dev')
All inputs are finite; a program needn't handle non-finite values.
Results may differ from a plain program's by a relative error of at most 0.001.
Values are sent between devices in bfloat16 or wider.
A program may use at most 1 GiB of HBM per device.

v0:
```python
import jax
import jax.numpy as jnp
from jax import lax
from jax.sharding import PartitionSpec as P


def solution(mesh):
    def local_part(ao_rows, c_occ, c_vir):
        n_rows = ao_rows.shape[0]
        n_ao = ao_rows.shape[1]
        n_occ = c_occ.shape[1]
        n_vir = c_vir.shape[1]
        quarter = jnp.einsum('pqrs,rx->pqsx', ao_rows, c_occ, preferred_element_type=jnp.float32).astype(jnp.bfloat16)
        half_oo = jnp.einsum('pqsx,sj->pqxj', quarter, c_occ, preferred_element_type=jnp.float32).astype(jnp.bfloat16)
        half_ov = jnp.einsum('pqsx,sb->pqxb', quarter, c_vir, preferred_element_type=jnp.float32).astype(jnp.bfloat16)
        half_oo = half_oo.reshape(n_rows, n_ao, n_occ * n_occ)
        half_ov = half_ov.reshape(n_rows, n_ao, n_occ * n_vir)
        full_oo = lax.all_to_all(half_oo, 'dev', 2, 0, tiled=True)
        full_ov = lax.all_to_all(half_ov, 'dev', 2, 0, tiled=True)
        mid_oo = jnp.einsum('qrn,rc->qcn', full_oo, c_vir, preferred_element_type=jnp.float32).astype(jnp.bfloat16)
        mid_ov = jnp.einsum('qrn,rb->qbn', full_ov, c_vir, preferred_element_type=jnp.float32).astype(jnp.bfloat16)
        v_abij = jnp.einsum('pa,pbm->abm', c_vir, mid_oo, preferred_element_type=jnp.float32)
        v_iajb = jnp.einsum('pi,pam->iam', c_occ, mid_ov, preferred_element_type=jnp.float32)
        return v_abij, v_iajb

    return jax.shard_map(local_part, mesh=mesh,
                         in_specs=(P(('frag', 'dev')), P('frag'), P('frag')),
                         out_specs=(P('frag', None, 'dev'), P('frag', None, 'dev')),
                         check_vma=False)
```

profile of v0, /device:TPU:0, one launch (start us, length us, event | category | flops | bytes accessed | tf_op | source)
XLA Modules:
  0.0 146.8 jit_solution(14483401578174017429)
XLA Ops:
  0.6 0.0 copy-start
  0.6 0.0 copy-start.2
  0.7 18.7 %convolution_convert_fusion = bf16[14,112,112,16]{2,3,1,0:T(8,128)(2,1)S(1)} fusion(bf16[14,112,112,112]{3,2,1,0:T(8,128)(2,1)} %param.3, bf16[112,16]{0,1:T(8,128)(2,1)} %param.4), kind=kOutput, calls=%fused_computation | convolution fusion | flops 632217600 | bytes 44961280 | tf_op jit(solution)/shard_map/pqrs,rx->pqsx/dot_general | solution.py:13
  19.4 0.0 copy-start.1
  19.4 2.7 %copy-done.1 = bf16[14,112,112,16]{2,3,1,0:T(8,128)(2,1)} copy-done((bf16[14,112,112,16]{2,3,1,0:T(8,128)(2,1)}, bf16[14,112,112,16]{2,3,1,0:T(8,128)(2,1)S(1)}, u32[]{:S(2)}) %copy-start.1) | copy-done | bytes 5619736
  22.1 0.0 copy-done.2
  22.1 3.7 %fusion.7 = bf16[14,112,16,16]{1,3,2,0:T(8,128)(2,1)S(1)} fusion(bf16[14,112,112,16]{2,3,1,0:T(8,128)(2,1)S(1)} %convolution_convert_fusion, bf16[112,16]{0,1:T(8,128)(2,1)S(1)} %copy-done.2), kind=kOutput, calls=%fused_computation.9 | convolution fusion | flops 90316800 | bytes 6426112 | tf_op jit(solution)/shard_map/pqsx,sj->pqxj/dot_general | solution.py:14
  25.8 1.6 %copy.22 = bf16[14,112,256]{1,0,2:T(8,128)(2,1)} copy(bf16[14,112,256]{1,2,0:T(8,128)(2,1)S(1)} %bitcast.48) | data formatting | bytes 1605632 | tf_op jit(solution)/shard_map/reshape | solution.py:16
  27.4 4.3 %all-to-all-start = ((bf16[14,112,256]{1,0,2:T(8,128)(2,1)}), bf16[14,112,256]{1,0,2:T(8,128)(2,1)S(1)}, u32[]{:S(2)}, u32[]{:S(2)}) async-start(bf16[14,112,256]{1,0,2:T(8,128)(2,1)} %copy.22), calls=%async_computation | async-start | bytes 2097152 | tf_op jit(solution)/shard_map/all_to_all | solution.py:18
  31.7 0.0 copy-done
  31.7 7.2 %fusion.4 = bf16[14,112,16,88]{1,3,2,0:T(8,128)(2,1)S(1)} fusion(bf16[14,112,112,16]{2,3,1,0:T(8,128)(2,1)} %copy-done.1, bf16[112,88]{0,1:T(8,128)(2,1)S(1)} %copy-done), kind=kOutput, calls=%fused_computation.6 | convolution fusion | flops 496742400 | bytes 10054912 | tf_op jit(solution)/shard_map/pqsx,sb->pqxb/dot_general | solution.py:15
  38.9 16.5 %copy.27 = bf16[14,112,1408]{1,0,2:T(8,128)(2,1)} copy(bf16[14,112,1408]{1,2,0:T(8,128)(2,1)S(1)} %bitcast.44) | data formatting | bytes 8830976 | tf_op jit(solution)/shard_map/reshape | solution.py:17
  55.4 0.0 all-to-all-done
  55.4 3.7 %all-to-all-start.1 = ((bf16[14,112,1408]{1,0,2:T(8,128)(2,1)}), bf16[14,112,1408]{1,0,2:T(8,128)(2,1)}, u32[]{:S(2)}, u32[]{:S(2)}) async-start(bf16[14,112,1408]{1,0,2:T(8,128)(2,1)} %copy.27), calls=%async_computation.1 | async-start | bytes 11534336 | tf_op jit(solution)/shard_map/all_to_all | solution.py:19
  59.1 0.2 copy.24
  59.3 0.9 convolution_bitcast_fusion
  60.3 2.1 %copy.31 = f32[88,88,32]{1,2,0:T(8,128)} copy(f32[88,88,32]{0,1,2:T(8,128)S(1)} %convolution_bitcast_fusion) | data formatting | bytes 1982464
  62.4 62.5 %all-to-all-done.1 = bf16[14,112,1408]{1,0,2:T(8,128)(2,1)} async-done(((bf16[14,112,1408]{1,0,2:T(8,128)(2,1)}), bf16[14,112,1408]{1,0,2:T(8,128)(2,1)}, u32[]{:S(2)}, u32[]{:S(2)}) %all-to-all-start.1) | async-done | bytes 4415520 | tf_op jit(solution)/shard_map/all_to_all | solution.py:19
  124.9 3.9 %copy.29 = bf16[8,14,112,176]{2,3,1,0:T(8,128)(2,1)S(1)} copy(bf16[8,14,112,176]{2,1,3,0:T(8,128)(2,1)} %bitcast.15) | data formatting | bytes 8830976 | tf_op jit(solution)/shard_map/all_to_all | solution.py:19
  128.9 3.2 %convert_bitcast_fusion = bf16[112,88,176]{1,2,0:T(8,128)(2,1)} fusion(bf16[112,112,176]{1,2,0:T(8,128)(2,1)S(1)} %bitcast.45, bf16[112,88]{0,1:T(8,128)(2,1)S(1)} %copy-done), kind=kOutput, calls=%fused_computation.5 | convolution fusion | flops 390297600 | bytes 7904512 | tf_op jit(solution)/shard_map/qrn,rb->qbn/dot_general | solution.py:21
  132.1 8.5 %copy.30 = bf16[112,88,176]{0,2,1:T(8,128)(2,1)} copy(bf16[112,88,176]{1,2,0:T(8,128)(2,1)} %convert_bitcast_fusion) | data formatting | bytes 6938624 | tf_op jit(solution)/shard_map/convert_element_type | solution.py:21
  140.6 4.3 %convolution_bitcast_fusion.1 = f32[16,88,176]{2,0,1:T(8,128)S(1)} fusion(bf16[112,88,176]{0,2,1:T(8,128)(2,1)} %copy.30, bf16[112,16]{0,1:T(8,128)(2,1)S(1)} %copy-done.2), kind=kOutput, calls=%fused_computation.8 | convolution fusion | flops 55508992 | bytes 4464128 | tf_op jit(solution)/shard_map/pi,pam->iam/dot_general | solution.py:23
  144.8 2.0 %copy.32 = f32[16,88,176]{2,1,0:T(8,128)} copy(f32[16,88,176]{2,0,1:T(8,128)S(1)} %convolution_bitcast_fusion.1) | data formatting | bytes 1982464
Async XLA Ops:
  0.6 31.1 %copy-start = (bf16[112,88]{0,1:T(8,128)(2,1)S(1)}, bf16[112,88]{0,1:T(8,128)(2,1)}, u32[]{:S(2)}) copy-start(bf16[112,88]{0,1:T(8,128)(2,1)} %param.5) | copy-start | bytes 59140
  0.6 21.4 %copy-start.2 = (bf16[112,16]{0,1:T(8,128)(2,1)S(1)}, bf16[112,16]{0,1:T(8,128)(2,1)}, u32[]{:S(2)}) copy-start(bf16[112,16]{0,1:T(8,128)(2,1)} %param.4) | copy-start | bytes 10756
  19.4 2.7 %copy-start.1 = (bf16[14,112,112,16]{2,3,1,0:T(8,128)(2,1)}, bf16[14,112,112,16]{2,3,1,0:T(8,128)(2,1)S(1)}, u32[]{:S(2)}) copy-start(bf16[14,112,112,16]{2,3,1,0:T(8,128)(2,1)S(1)} %convolution_convert_fusion) | copy-start | bytes 16859140
  27.4 28.0 %all-to-all-start = ((bf16[14,112,256]{1,0,2:T(8,128)(2,1)}), bf16[14,112,256]{1,0,2:T(8,128)(2,1)S(1)}, u32[]{:S(2)}, u32[]{:S(2)}) async-start(bf16[14,112,256]{1,0,2:T(8,128)(2,1)} %copy.22), calls=%async_computation | async-start | bytes 2097152 | tf_op jit(solution)/shard_map/all_to_all | solution.py:18
  55.4 69.5 %all-to-all-start.1 = ((bf16[14,112,1408]{1,0,2:T(8,128)(2,1)}), bf16[14,112,1408]{1,0,2:T(8,128)(2,1)}, u32[]{:S(2)}, u32[]{:S(2)}) async-start(bf16[14,112,1408]{1,0,2:T(8,128)(2,1)} %copy.27), calls=%async_computation.1 | async-start | bytes 11534336 | tf_op jit(solution)/shard_map/all_to_all | solution.py:19
where the time goes:
time: 147 us
  waiting for transfers between devices  62.5 us (43%)
  matrix products  38 us (26%)
  local copies, waits for them, and re-layouts  37.6 us (26%)
  starting transfers between devices  7.97 us (5%)
    all_to_all x1, waiting for transfers between devices, local_part(): full_ov = lax.all_to_all(half_ov, 'dev', 2, 0, tiled=True)  62.5 us
    dot_general x1, matrix products, local_part(): jnp.einsum('pqrs,rx->pqsx', ao_rows, c_occ, preferred_element_type=jnp.fl...  18.7 us
    reshape x1, local copies, waits for them, and re-layouts, local_part(): half_ov = half_ov.reshape(n_rows, n_ao, n_occ * n_vir)  16.5 us
    convert_element_type x1, local copies, waits for them, and re-layouts, local_part(): jnp.einsum('qrn,rb->qbn', full_ov, c_vir, preferred_element_type=jnp.floa...  8.49 us
    dot_general x1, matrix products, local_part(): jnp.einsum('pqsx,sb->pqxb', quarter, c_vir, preferred_element_type=jnp.fl...  7.16 us
    unnamed x8, local copies, waits for them, and re-layouts  6.8 us
    all_to_all x1, starting transfers between devices, local_part(): full_oo = lax.all_to_all(half_oo, 'dev', 2, 0, tiled=True)  4.31 us
    dot_general x1, matrix products, local_part(): jnp.einsum('pi,pam->iam', c_occ, mid_ov, preferred_element_type=jnp.float32)  4.27 us
  transfers between devices with their start and end apart: 2, of which 1 were waited for; matrix products, arithmetic and copies ran while one was open for 18% of the time, Pallas kernels for 0%

commit v1 on v0

v1 whole, which is shorter than its diff:
```python
import functools

import jax
import jax.numpy as jnp
from jax import lax
from jax.experimental import pallas as pl
from jax.experimental.pallas import tpu as pltpu
from jax.sharding import PartitionSpec as P

MESH = pl.DeviceIdType.MESH
F32 = jnp.float32
BF16 = jnp.bfloat16


def dot(a, b):
    return jnp.dot(a, b, preferred_element_type=F32)


def iota(shape, d):
    return lax.broadcasted_iota(jnp.int32, shape, d)


def onehot(cond):
    return jnp.where(cond, 1.0, 0.0).astype(BF16)


def kernel(nd, np_, n, no, nv, a_ref, co_ref, cv_ref, v1_ref, v2_ref,
           a_buf, t_buf, w_buf, cot, cvt, s_buf, r_buf, l1_buf, l2_buf,
           a_sem, send_sem, recv_sem):
    me = lax.axis_index("dev")
    frag = lax.axis_index("frag")
    nab = nv // 8

    def a_copy(p):
        slot = lax.rem(p, 2)
        return pltpu.make_async_copy(a_ref.at[p], a_buf.at[slot], a_sem.at[slot])

    a_copy(0).start()

    barrier = pltpu.get_barrier_semaphore()
    for k in range(1, nd):
        pl.semaphore_signal(barrier, inc=1, device_id=(frag, lax.rem(me + k, nd)), device_id_type=MESH)

    co = co_ref[...]
    cv = cv_ref[...]
    eye = onehot(iota((n, n), 0) == iota((n, n), 1))
    tdims = (((0,), (0,)), ((), ()))
    cot[...] = lax.dot_general(co, eye, tdims, preferred_element_type=F32).astype(BF16)
    cvt[...] = lax.dot_general(cv, eye, tdims, preferred_element_type=F32).astype(BF16)
    w_buf[...] = jnp.zeros_like(w_buf)
    t_buf[...] = jnp.zeros_like(t_buf)
    for j in range(2):
        b = iota((nv, 256), 0) + j * nv
        c = iota((nv, 256), 1)
        sel_v = onehot(c == jnp.where(b < 128, b, b + 32))
        jj = iota((no, 256), 0) + 128 + no * j
        sel_o = onehot(iota((no, 256), 1) == jj)
        w_buf[128 * j:128 * j + n, :] = (dot(cv, sel_v) + dot(co, sel_o)).astype(BF16)

    pl.semaphore_wait(barrier, nd - 1)

    def remote(p, k):
        d = lax.rem(me + k, nd)
        return pltpu.make_async_remote_copy(
            src_ref=s_buf.at[p, k], dst_ref=r_buf.at[p, me],
            send_sem=send_sem.at[p, k], recv_sem=recv_sem.at[p, me],
            device_id=(frag, d), device_id_type=MESH)

    def row(p, _):
        slot = lax.rem(p, 2)
        a_copy(p).wait()

        @pl.when(p + 1 < np_)
        def _():
            a_copy(p + 1).start()

        UQ = 8

        def step1(g, _):
            for u in range(UQ):
                q = g * UQ + u
                t = dot(cot[...], a_buf[slot, q])
                t_buf[pl.ds(q * no, no), 0:n] = t
            return 0

        lax.fori_loop(0, n // UQ, step1, 0)

        def step23(k):
            d = lax.rem(me + k, nd)
            t0 = t_buf[pl.ds(2 * d, n, stride=no), :].astype(BF16)
            t1 = t_buf[pl.ds(2 * d + 1, n, stride=no), :].astype(BF16)
            h = dot(jnp.concatenate([t0, t1], axis=1), w_buf[...]).astype(BF16)
            return dot(cvt[...], h).astype(BF16).reshape(nab, 8, 256)

        def dest(k, _):
            s_buf[p, k] = step23(k)
            remote(p, k).start()
            return 0

        lax.fori_loop(1, nd, dest, 0)
        r_buf[p, me] = step23(0)
        return 0

    lax.fori_loop(0, np_, row, 0)

    PB = 4
    for lo in range(0, np_, PB):
        pb = min(PB, np_ - lo)
        kk = pb * nd * 8
        k_i = iota((n, kk), 1)
        perm = onehot(iota((n, kk), 0) == np_ * ((k_i // 8) % nd) + lo + k_i // (8 * nd))
        for m, tab, out in ((no, cot, l2_buf), (nv, cvt, l1_buf)):
            rep = onehot(iota((m * 8, m), 0) // 8 == iota((m * 8, m), 1))
            x = dot(tab[...], perm).astype(BF16)
            x = dot(rep, x)
            same = (iota((m * 8, kk), 0) % 8) == (iota((m * 8, kk), 1) % 8)
            out[:, 0:kk] = jnp.where(same, x, 0.0).astype(BF16)

        def wait_one(idx, _):
            p = lo + idx // (nd - 1)
            src = lax.rem(me + 1 + lax.rem(idx, nd - 1), nd)
            pltpu.make_async_remote_copy(
                src_ref=s_buf.at[p, 1], dst_ref=r_buf.at[p, src],
                send_sem=send_sem.at[p, 1], recv_sem=recv_sem.at[p, src],
                device_id=(frag, src), device_id_type=MESH).wait_recv()
            return 0

        lax.fori_loop(0, pb * (nd - 1), wait_one, 0)

        def block(ab, _):
            r = r_buf[lo:lo + pb, :, ab].reshape(kk, 256)
            o2 = dot(l2_buf[:, 0:kk], r).reshape(no, 8, 256)
            o1 = dot(l1_buf[:, 0:kk], r[:, 128:256]).reshape(nv, 8, 128)
            rows = pl.ds(pl.multiple_of(ab * 8, 8), 8)
            if lo == 0:
                v2_ref[:, rows, 0:128] = o2[:, :, 0:128]
                v2_ref[:, rows, 128:176] = o2[:, :, 160:208]
                v1_ref[:, rows, :] = o1[:, :, 0:32]
            else:
                v2_ref[:, rows, 0:128] += o2[:, :, 0:128]
                v2_ref[:, rows, 128:176] += o2[:, :, 160:208]
                v1_ref[:, rows, :] += o1[:, :, 0:32]
            return 0

        lax.fori_loop(0, nab, block, 0)

    def drain(idx, _):
        p = idx // (nd - 1)
        k = 1 + lax.rem(idx, nd - 1)
        remote(p, k).wait_send()
        return 0

    lax.fori_loop(0, np_ * (nd - 1), drain, 0)


def solution(mesh):
    nd = mesh.shape["dev"]

    def local_part(a, co, cv):
        np_, n = a.shape[0], a.shape[1]
        no, nv = co.shape[1], cv.shape[1]
        vm = pl.BlockSpec(memory_space=pltpu.VMEM)
        return pl.pallas_call(
            functools.partial(kernel, nd, np_, n, no, nv),
            out_shape=(jax.ShapeDtypeStruct((nv, nv, no * no // nd), F32),
                       jax.ShapeDtypeStruct((no, nv, no * nv // nd), F32)),
            in_specs=[pl.BlockSpec(memory_space=pl.ANY), vm, vm],
            out_specs=(vm, vm),
            scratch_shapes=[
                pltpu.VMEM((2, n, n, n), BF16),
                pltpu.VMEM((n * no, 128), F32),
                pltpu.VMEM((256, 256), BF16),
                pltpu.VMEM((no, n), BF16),
                pltpu.VMEM((nv, n), BF16),
                pltpu.VMEM((np_, nd, nv // 8, 8, 256), BF16),
                pltpu.VMEM((np_, nd, nv // 8, 8, 256), BF16),
                pltpu.VMEM((nv * 8, 256), BF16),
                pltpu.VMEM((no * 8, 256), BF16),
                pltpu.SemaphoreType.DMA((2,)),
                pltpu.SemaphoreType.DMA((np_, nd)),
                pltpu.SemaphoreType.DMA((np_, nd)),
            ],
            compiler_params=pltpu.CompilerParams(
                collective_id=0, has_side_effects=True, vmem_limit_bytes=60 * 1024 * 1024),
        )(a, co, cv)

    return jax.shard_map(local_part, mesh=mesh,
                         in_specs=(P(('frag', 'dev')), P('frag'), P('frag')),
                         out_specs=(P('frag', None, 'dev'), P('frag', None, 'dev')),
                         check_vma=False)
```

time: 147 us -> 106 us (0.72)
  Pallas kernels: 0 us -> 97 us
  waiting for transfers between devices: 62.5 us -> 0 us
  matrix products: 38 us -> 0 us
  local copies, waits for them, and re-layouts: 37.6 us -> 7.62 us
  starting transfers between devices: 7.97 us -> 0 us
    pallas_call x0 -> x1, Pallas kernels: none -> 97 us  [local_part(): pl.pallas_call(functools.partial(kernel, nd, np_, n, no, nv), out_shape=(...]
    all_to_all x2 -> x0, waiting for transfers between devices: 62.5 us -> none  [the longest x1 62.5 us: local_part(): full_ov = lax.all_to_all(half_ov, 'dev', 2, 0, tiled=True)]
    dot_general x6 -> x0, matrix products: 38 us -> none  [the longest x1 18.7 us: local_part(): jnp.einsum('pqrs,rx->pqsx', ao_rows, c_occ, preferred_element_type=jnp.fl...]
    reshape x2 -> x0, local copies, waits for them, and re-layouts: 18.1 us -> none  [the longest x1 16.5 us: local_part(): half_ov = half_ov.reshape(n_rows, n_ao, n_occ * n_vir)]
    convert_element_type x1 -> x0, local copies, waits for them, and re-layouts: 8.49 us -> none  [local_part(): jnp.einsum('qrn,rb->qbn', full_ov, c_vir, preferred_element_type=jnp.floa...]
    all_to_all x2 -> x0, starting transfers between devices: 7.97 us -> none  [the longest x1 4.31 us: local_part(): full_oo = lax.all_to_all(half_oo, 'dev', 2, 0, tiled=True)]
    all_to_all x2 -> x0, local copies, waits for them, and re-layouts: 4.17 us -> none  [the longest x1 3.93 us: local_part(): full_ov = lax.all_to_all(half_ov, 'dev', 2, 0, tiled=True)]
    pallas_call x0 -> x1, local copies, waits for them, and re-layouts: none -> 3.68 us  [local_part(): pl.pallas_call(functools.partial(kernel, nd, np_, n, no, nv), out_shape=(...]
  transfers between devices with their start and end apart: 2 -> 0, of which waited for: 1 -> 0; matrix products, arithmetic and copies ran while one was open for 18% -> 0% of each run, Pallas kernels for 0% -> 0%
where the time goes in v1:
time: 106 us; the launch traced here: 105 us
  Pallas kernels  97 us (92%)
  local copies, waits for them, and re-layouts  7.62 us (7%)
    pallas_call x1, Pallas kernels, local_part(): pl.pallas_call(functools.partial(kernel, nd, np_, n, no, nv), out_shape=(...  97 us
    unnamed x5, local copies, waits for them, and re-layouts  3.94 us
    pallas_call x1, local copies, waits for them, and re-layouts, local_part(): pl.pallas_call(functools.partial(kernel, nd, np_, n, no, nv), out_shape=(...  3.68 us

profile of v1, /device:TPU:0, one launch (start us, length us, event | category | flops | bytes accessed | tf_op | source)
XLA Modules:
  0.0 105.3 jit_solution(8286336177487726095)
XLA Ops:
  0.6 1.4 %copy.5.co_ref = bf16[112,16]{1,0:T(8,128)(2,1)} copy(bf16[112,16]{0,1:T(8,128)(2,1)} %param.4) | data formatting | bytes 7168 | tf_op args[1]
  2.0 1.4 %copy.6.cv_ref = bf16[112,88]{1,0:T(8,128)(2,1)} copy(bf16[112,88]{0,1:T(8,128)(2,1)} %param.5) | data formatting | bytes 39424 | tf_op args[2]
  3.5 97.0 %shard_map.50 = (f32[88,88,32]{2,1,0:T(8,128)}, f32[16,88,176]{2,1,0:T(8,128)}) custom-call(bf16[14,112,112,112]{3,2,1,0:T(8,128)(2,1)} %a_ref.1, bf16[112,16]{1,0:T(8,128)(2,1)} %copy.5.co_ref, bf16[112,88]{1,0:T(8,128)(2,1)} %copy.6.cv_ref), custom_call_target="tpu_custom_call" | custom-call | tf_op jit(solution)/shard_map/pallas_call | solution.py:163
  100.5 0.0 copy-start
  100.5 3.7 %copy.7 = f32[88,88,32]{1,2,0:T(8,128)} copy(f32[88,88,32]{2,1,0:T(8,128)} %get-tuple-element.2) | data formatting | bytes 1982464 | tf_op jit(solution)/shard_map/pallas_call | solution.py:163
  104.2 0.0 copy-done
  104.2 1.1 %copy.9 = f32[16,88,176]{2,1,0:T(8,128)} copy(f32[16,88,176]{2,1,0:T(8,128)S(1)} %copy-done) | data formatting | bytes 1982464
Async XLA Ops:
  100.5 3.7 %copy-start = (f32[16,88,176]{2,1,0:T(8,128)S(1)}, f32[16,88,176]{2,1,0:T(8,128)}, u32[]{:S(2)}) copy-start(f32[16,88,176]{2,1,0:T(8,128)} %get-tuple-element.7) | copy-start | bytes 2973700

commit v2 on v0

v2 whole, which is shorter than its diff:
```python
import functools

import jax
import jax.numpy as jnp
from jax import lax
from jax.experimental import pallas as pl
from jax.experimental.pallas import tpu as pltpu
from jax.sharding import PartitionSpec as P

MESH = pl.DeviceIdType.MESH
F32 = jnp.float32
BF16 = jnp.bfloat16
NX = 6
LAG = 3


def dot(a, b):
    return jnp.dot(a, b, preferred_element_type=F32)


def dot_t(a, b):
    return lax.dot_general(a, b, (((0,), (0,)), ((), ())), preferred_element_type=F32)


def iota(shape, d):
    return lax.broadcasted_iota(jnp.int32, shape, d)


def onehot(cond):
    return jnp.where(cond, 1.0, 0.0).astype(BF16)


def kernel(np_, n, no, nv, a_ref, cot_ref, cvt_ref, v1_ref, v2_ref,
           a_buf, la, ww, cv_buf, t_buf, h_buf, lx, ly, l1,
           sx, sy, so, rx, ry, ro, px, py, qx, qy,
           a_sem, sx_sem, sy_sem, so_sem, rx_sem, ry_sem, ro_sem,
           px_sem, py_sem, qx_sem, qy_sem):
    nd = 8
    npair = np_ // 2
    nb = nv // 8
    NY = nb - NX
    ng = n // 16
    me = lax.axis_index("dev")
    frag = lax.axis_index("frag")
    y, x, c = me // 4, (me // 2) % 2, me % 2

    def dev(k):
        dy, dx, dc = k
        return (1 - y if dy else y) * 4 + (1 - x if dx else x) * 2 + (1 - c if dc else c)

    def did(k):
        return (frag, dev(k))

    KS = [(1, 1, 0), (1, 1, 1), (1, 0, 1), (0, 1, 1), (1, 0, 0), (0, 1, 0), (0, 0, 1), (0, 0, 0)]

    def a_copy(p, g):
        slot = p % 4
        return pltpu.make_async_copy(a_ref.at[p, pl.ds(16 * g, 16)], a_buf.at[slot, pl.ds(16 * g, 16)],
                                     a_sem.at[slot, g])

    for p in range(2):
        for g in range(ng):
            a_copy(p, g).start()

    barrier = pltpu.get_barrier_semaphore()
    for k in KS[:-1]:
        pl.semaphore_signal(barrier, inc=1, device_id=did(k), device_id_type=MESH)

    cot = cot_ref[...]
    cvt = cvt_ref[...]
    co = dot_t(cot, onehot(iota((no, no), 0) == iota((no, no), 1))).astype(BF16)
    cv = dot_t(cvt, onehot(iota((nv, nv), 0) == iota((nv, nv), 1))).astype(BF16)
    cv_buf[...] = cv
    rep8 = onehot(iota((no * 8, no), 0) // 8 == iota((no * 8, no), 1))
    tile = onehot(iota((n, 8 * n), 0) == iota((n, 8 * n), 1) % n)
    m = dot(rep8, dot(cot, tile).astype(BF16))
    la[...] = jnp.where(iota(m.shape, 0) % 8 == iota(m.shape, 1) // n, m, 0.0).astype(BF16)
    ww[...] = jnp.zeros_like(ww)
    for par in range(2):
        for j in range(2):
            jb = iota((nv, 512), 0) + j * nv
            col = iota((nv, 512), 1)
            sel_v = onehot(col == jnp.where(jb < 128, par * 128 + jb, 256 + 48 * par + jb - 128))
            sel_o = onehot(iota((no, 512), 1) == iota((no, 512), 0) + 384 + 32 * par + no * j)
            r0 = 256 * par + 128 * j
            ww[r0:r0 + n, :] = (dot(cv, sel_v) + dot(co, sel_o)).astype(BF16)

    for p in range(2, 4):
        for g in range(ng):
            a_copy(p, g).start()

    def kron(tab, m_, kk, p_of_col, same):
        perm = onehot(iota((n, kk), 0) == p_of_col(iota((n, kk), 1)))
        r = onehot(iota((m_ * 8, m_), 0) // 8 == iota((m_ * 8, m_), 1))
        v = dot(r, dot(tab, perm).astype(BF16))
        return jnp.where(iota(v.shape, 0) % 8 == same(iota(v.shape, 1)), v, 0.0).astype(BF16)

    k4 = npair * 32
    for par in range(2):
        lx[par] = kron(cot, no, k4, lambda t: np_ * (y * 4 + (t // 8) % 4) + 2 * (t // 32) + par, lambda t: t % 8)
        ly[par] = kron(cot, no, k4, lambda t: np_ * ((t // 16) % 2 * 4 + x * 2 + (t // 8) % 2) + 2 * (t // 32) + par,
                       lambda t: t % 8)

    pl.semaphore_wait(barrier, nd - 1)

    def send_x(i, k):
        h = (0, k[1], k[2])
        return pltpu.make_async_remote_copy(
            src_ref=sx.at[i, dev(k)], dst_ref=rx.at[i, x * 2 + c, k[0]],
            send_sem=sx_sem.at[i, dev(k)], recv_sem=rx_sem.at[i, x * 2 + c, k[0]],
            device_id=did(h), device_id_type=MESH)

    def send_y(i, k):
        h = (k[0], 0, k[2])
        return pltpu.make_async_remote_copy(
            src_ref=sy.at[i, dev(k)], dst_ref=ry.at[i, y * 2 + c, k[1]],
            send_sem=sy_sem.at[i, dev(k)], recv_sem=ry_sem.at[i, y * 2 + c, k[1]],
            device_id=did(h), device_id_type=MESH)

    def send_o(i, k):
        return pltpu.make_async_remote_copy(
            src_ref=so.at[i, dev(k)], dst_ref=ro.at[i, me],
            send_sem=so_sem.at[i, dev(k)], recv_sem=ro_sem.at[i, me],
            device_id=did(k), device_id_type=MESH)

    def far_x(k):
        return bool(k[1] or k[2])

    def far_y(k):
        return bool(k[0] or k[2])

    def send_relay(i):
        for k in KS:
            if far_x(k) and k[0]:
                send_x(i, k).start()
            if far_y(k) and k[1]:
                send_y(i, k).start()

    def send_direct(i):
        for k in KS:
            if far_x(k) and not k[0]:
                send_x(i, k).start()
            if far_y(k) and not k[1]:
                send_y(i, k).start()
            if k != (0, 0, 0):
                send_o(i, k).start()

    zpad = jnp.zeros((8 * n, 128 - n), BF16)

    def pair(i, _):
        for par in range(2):
            p = 2 * i + par
            slot = p % 4

            def step1(g, _):
                a_copy(p, g).wait()
                a0 = a_buf[slot, pl.ds(16 * g, 8)].reshape(8 * n, n)
                a1 = a_buf[slot, pl.ds(16 * g + 8, 8)].reshape(8 * n, n)
                w = jnp.concatenate([a0, zpad, a1, zpad], axis=1)
                t = dot(la[...], w)
                rows = pl.ds(pl.multiple_of(16 * g, 16), 16)
                for xx in range(no):
                    tx = t[8 * xx:8 * xx + 8]
                    tx = jnp.concatenate([tx[:, 0:128], tx[:, 128:256]], axis=0).astype(BF16)
                    l0 = par * 256 + (xx % 2) * 128
                    t_buf[xx // 2, rows, l0:l0 + 128] = tx
                return 0

            lax.fori_loop(0, ng, step1, 0)

            @pl.when(p + 4 < np_)
            def _():
                for g in range(ng):
                    a_copy(p + 4, g).start()

        def step2(d, _):
            tt = t_buf[pl.ds(4 * d, 4)].reshape(4 * n, 512)
            h_buf[pl.ds(4 * d, 4)] = dot(tt, ww[...]).astype(BF16).reshape(4, n, 512)
            return 0

        lax.fori_loop(0, 2, step2, 0)

        for k in KS:
            d = dev(k)
            h = h_buf[d]
            g = dot(cvt_ref[...], h[:, 0:384]).astype(BF16).reshape(nb, 8, 384)
            if far_x(k):
                sx[i, d] = g[0:NX]
            else:
                rx[i, x * 2 + c, k[0]] = g[0:NX]
            if far_y(k):
                sy[i, d] = g[NX:nb]
            else:
                ry[i, y * 2 + c, k[1]] = g[NX:nb]
            go = dot_t(h[:, 384:384 + 4 * no], cv_buf[...]).astype(BF16)
            if k == (0, 0, 0):
                ro[i, me] = go
            else:
                so[i, d] = go

        send_relay(i)

        @pl.when(i >= LAG)
        def _():
            send_direct(i - LAG)

        return 0

    lax.fori_loop(0, npair, pair, 0)
    for i in range(npair - LAG, npair):
        send_direct(i)

    def wait_x(i, sc, w):
        pltpu.make_async_remote_copy(
            src_ref=rx.at[i, sc, w], dst_ref=rx.at[i, sc, w], send_sem=sx_sem.at[0, 0],
            recv_sem=rx_sem.at[i, sc, w], device_id=did((0, 0, 1)), device_id_type=MESH).wait_recv()

    def wait_y(i, sc, w):
        pltpu.make_async_remote_copy(
            src_ref=ry.at[i, sc, w], dst_ref=ry.at[i, sc, w], send_sem=sy_sem.at[0, 0],
            recv_sem=ry_sem.at[i, sc, w], device_id=did((0, 0, 1)), device_id_type=MESH).wait_recv()

    def wait_o(i, src):
        pltpu.make_async_remote_copy(
            src_ref=ro.at[i, src], dst_ref=ro.at[i, src], send_sem=so_sem.at[0, 0],
            recv_sem=ro_sem.at[i, src], device_id=did((0, 0, 1)), device_id_type=MESH).wait_recv()

    def wait_v2(w):
        def body(i, _):
            for e in range(1, 4):
                wait_x(i, (x * 2 + c + e) % 4, w)
                wait_y(i, (y * 2 + c + e) % 4, w)
            return 0
        lax.fori_loop(0, npair, body, 0)

    def partial(r, left, w, ab):
        v = r[:, :, w, ab].reshape(k4, 384)
        main = dot(left[0], v[:, 0:128]) + dot(left[1], v[:, 128:256])
        even = dot(left[0], v[:, 256:384])
        odd = dot(left[1], v[:, 256:384])
        return main.reshape(no, 8, 128), even.reshape(no, 8, 128), odd.reshape(no, 8, 128)

    lane = iota((8, 8, 128), 2)

    def send_p(buf, out, ssem, rsem, h, ab):
        return pltpu.make_async_remote_copy(
            src_ref=buf.at[ab], dst_ref=out.at[ab], send_sem=ssem.at[ab], recv_sem=rsem.at[ab],
            device_id=did(h), device_id_type=MESH)

    wait_v2(1)
    for r, left, buf, out, ssem, rsem, h, cnt in (
            (rx, lx, px, qx, px_sem, qx_sem, (1, 0, 0), NX), (ry, ly, py, qy, py_sem, qy_sem, (0, 1, 0), NY)):
        def relay(ab, _, r=r, left=left, buf=buf, out=out, ssem=ssem, rsem=rsem, h=h):
            main, even, odd = partial(r, left, 1, ab)
            buf[ab, 0:no] = main
            lo = even[0:8] + pltpu.roll(odd[0:8], 80, 2)
            hi = pltpu.roll(even[8:16], 48, 2) + odd[8:16]
            buf[ab, no:no + 8] = jnp.where(lane < 48, lo, hi)
            send_p(buf, out, ssem, rsem, h, ab).start()
            return 0
        lax.fori_loop(0, cnt, relay, 0)

    wait_v2(0)
    for r, left, cnt, base in ((rx, lx, NX, 0), (ry, ly, NY, NX)):
        def own(ab, _, r=r, left=left, base=base):
            main, even, odd = partial(r, left, 0, ab)
            rows = pl.ds(pl.multiple_of((ab + base) * 8, 8), 8)
            v2_ref[:, rows, 0:128] = main
            v2_ref[:, rows, 128:176] = (even + pltpu.roll(odd, 80, 2))[:, :, 0:48]
            return 0
        lax.fori_loop(0, cnt, own, 0)

    k8 = npair * 128
    l1[...] = kron(cvt_ref[...], nv, k8,
                   lambda t: np_ * ((t // 16) % 8) + 2 * (t // 128) + (t // 8) % 2, lambda t: t % 8)

    def wait_oo(i, _):
        for e in range(1, nd):
            wait_o(i, (me + e) % nd)
        return 0
    lax.fori_loop(0, npair, wait_oo, 0)

    for ib in range(4):
        def oo_rows(par):
            return ro[:, :, par * 32 + 8 * ib:par * 32 + 8 * ib + 8].reshape(npair * nd, 8, nv)
        w = jnp.concatenate([oo_rows(0), oo_rows(1)], axis=1).reshape(k8, nv)
        v1_ref[:, 8 * ib:8 * ib + 8, :] = dot(l1[...], w).reshape(nv, 8, nv)

    for buf, out, ssem, rsem, h, cnt, base in (
            (px, qx, px_sem, qx_sem, (1, 0, 0), NX, 0), (py, qy, py_sem, qy_sem, (0, 1, 0), NY, NX)):
        def add(ab, _, buf=buf, out=out, ssem=ssem, rsem=rsem, h=h, base=base):
            send_p(buf, out, ssem, rsem, h, ab).wait()
            rows = pl.ds(pl.multiple_of((ab + base) * 8, 8), 8)
            v2_ref[:, rows, 0:128] += out[ab, 0:no]
            ext = out[ab, no:no + 8]
            v2_ref[0:8, rows, 128:176] += ext[:, :, 0:48]
            v2_ref[8:16, rows, 128:176] += pltpu.roll(ext, 80, 2)[:, :, 0:48]
            return 0
        lax.fori_loop(0, cnt, add, 0)

    def drain(i, _):
        for k in KS:
            if far_x(k):
                send_x(i, k).wait_send()
            if far_y(k):
                send_y(i, k).wait_send()
            if k != (0, 0, 0):
                send_o(i, k).wait_send()
        return 0
    lax.fori_loop(0, npair, drain, 0)


def solution(mesh):
    nd = mesh.shape["dev"]

    def local_part(a, co, cv):
        np_, n = a.shape[0], a.shape[1]
        no, nv = co.shape[1], cv.shape[1]
        npair, nb = np_ // 2, nv // 8
        ny = nb - NX
        vm = pl.BlockSpec(memory_space=pltpu.VMEM)
        dma = pltpu.SemaphoreType.DMA
        v1, v2 = pl.pallas_call(
            functools.partial(kernel, np_, n, no, nv),
            out_shape=(jax.ShapeDtypeStruct((nv, no * no // nd, nv), F32),
                       jax.ShapeDtypeStruct((no, nv, no * nv // nd), F32)),
            in_specs=[pl.BlockSpec(memory_space=pl.ANY), vm, vm],
            out_specs=(vm, vm),
            scratch_shapes=[
                pltpu.VMEM((4, n, n, n), BF16),
                pltpu.VMEM((no * 8, n * 8), BF16),
                pltpu.VMEM((512, 512), BF16),
                pltpu.VMEM((n, nv), BF16),
                pltpu.VMEM((nd, n, 512), BF16),
                pltpu.VMEM((nd, n, 512), BF16),
                pltpu.VMEM((2, no * 8, npair * 32), BF16),
                pltpu.VMEM((2, no * 8, npair * 32), BF16),
                pltpu.VMEM((nv * 8, npair * 128), BF16),
                pltpu.VMEM((npair, nd, NX, 8, 384), BF16),
                pltpu.VMEM((npair, nd, ny, 8, 384), BF16),
                pltpu.VMEM((npair, nd, 4 * no, nv), BF16),
                pltpu.VMEM((npair, 4, 2, NX, 8, 384), BF16),
                pltpu.VMEM((npair, 4, 2, ny, 8, 384), BF16),
                pltpu.VMEM((npair, nd, 4 * no, nv), BF16),
                pltpu.VMEM((NX, no + 8, 8, 128), F32),
                pltpu.VMEM((ny, no + 8, 8, 128), F32),
                pltpu.VMEM((NX, no + 8, 8, 128), F32),
                pltpu.VMEM((ny, no + 8, 8, 128), F32),
                dma((4, n // 16)),
                dma((npair, nd)), dma((npair, nd)), dma((npair, nd)),
                dma((npair, 4, 2)), dma((npair, 4, 2)), dma((npair, nd)),
                dma((NX,)), dma((ny,)), dma((NX,)), dma((ny,)),
            ],
            compiler_params=pltpu.CompilerParams(
                collective_id=0, has_side_effects=True, vmem_limit_bytes=60 * 1024 * 1024),
        )(a, co.T, cv.T)
        return v1.transpose(0, 2, 1), v2

    return jax.shard_map(local_part, mesh=mesh,
                         in_specs=(P(('frag', 'dev')), P('frag'), P('frag')),
                         out_specs=(P('frag', None, 'dev'), P('frag', None, 'dev')),
                         check_vma=False)
```

time: 147 us -> 74.3 us (0.51)
  Pallas kernels: 0 us -> 69.7 us
  waiting for transfers between devices: 62.5 us -> 0 us
  matrix products: 38 us -> 0 us
  local copies, waits for them, and re-layouts: 37.6 us -> 3.78 us
  starting transfers between devices: 7.97 us -> 0 us
    pallas_call x0 -> x1, Pallas kernels: none -> 69.7 us  [local_part(): pl.pallas_call(functools.partial(kernel, np_, n, no, nv), out_shape=(jax....]
    all_to_all x2 -> x0, waiting for transfers between devices: 62.5 us -> none  [the longest x1 62.5 us: local_part(): full_ov = lax.all_to_all(half_ov, 'dev', 2, 0, tiled=True)]
    dot_general x6 -> x0, matrix products: 38 us -> none  [the longest x1 18.7 us: local_part(): jnp.einsum('pqrs,rx->pqsx', ao_rows, c_occ, preferred_element_type=jnp.fl...]
    reshape x2 -> x0, local copies, waits for them, and re-layouts: 18.1 us -> none  [the longest x1 16.5 us: local_part(): half_ov = half_ov.reshape(n_rows, n_ao, n_occ * n_vir)]
    convert_element_type x1 -> x0, local copies, waits for them, and re-layouts: 8.49 us -> none  [local_part(): jnp.einsum('qrn,rb->qbn', full_ov, c_vir, preferred_element_type=jnp.floa...]
    all_to_all x2 -> x0, starting transfers between devices: 7.97 us -> none  [the longest x1 4.31 us: local_part(): full_oo = lax.all_to_all(half_oo, 'dev', 2, 0, tiled=True)]
    all_to_all x2 -> x0, local copies, waits for them, and re-layouts: 4.17 us -> none  [the longest x1 3.93 us: local_part(): full_ov = lax.all_to_all(half_ov, 'dev', 2, 0, tiled=True)]
    unnamed x8 -> x4, local copies, waits for them, and re-layouts: 6.8 us -> 3.78 us
  transfers between devices with their start and end apart: 2 -> 0, of which waited for: 1 -> 0; matrix products, arithmetic and copies ran while one was open for 18% -> 0% of each run, Pallas kernels for 0% -> 0%
where the time goes in v2:
time: 74.3 us; the launch traced here: 74.1 us
  Pallas kernels  69.7 us (94%)
  local copies, waits for them, and re-layouts  3.78 us (5%)
    pallas_call x1, Pallas kernels, local_part(): pl.pallas_call(functools.partial(kernel, np_, n, no, nv), out_shape=(jax....  69.7 us
    unnamed x4, local copies, waits for them, and re-layouts  3.78 us

profile of v2, /device:TPU:0, one launch (start us, length us, event | category | flops | bytes accessed | tf_op | source)
XLA Modules:
  0.0 74.1 jit_solution(17638335834661969555)
XLA Ops:
  0.6 69.7 %shard_map.50 = (f32[88,32,88]{2,1,0:T(8,128)}, f32[16,88,176]{2,1,0:T(8,128)}) custom-call(bf16[14,112,112,112]{3,2,1,0:T(8,128)(2,1)} %a_ref.1, bf16[16,112]{1,0:T(8,128)(2,1)} %bitcast.5, bf16[88,112]{1,0:T(8,128)(2,1)} %bitcast.4), custom_call_target="tpu_custom_call" | custom-call | tf_op jit(solution)/shard_map/pallas_call | solution.py:323
  70.3 0.0 copy-start
  70.3 2.7 %copy.7 = f32[88,88,32]{1,2,0:T(8,128)} copy(f32[88,88,32]{1,2,0:T(8,128)} %bitcast.3) | data formatting | bytes 1982464
  73.0 0.0 copy-done
  73.0 1.1 %copy.8 = f32[16,88,176]{2,1,0:T(8,128)} copy(f32[16,88,176]{2,1,0:T(8,128)S(1)} %copy-done) | data formatting | bytes 1982464
Async XLA Ops:
  70.3 2.7 %copy-start = (f32[16,88,176]{2,1,0:T(8,128)S(1)}, f32[16,88,176]{2,1,0:T(8,128)}, u32[]{:S(2)}) copy-start(f32[16,88,176]{2,1,0:T(8,128)} %get-tuple-element.9) | copy-start | bytes 2973700

commit v3 on v2

v3 whole, which is shorter than its diff:
```python
import functools

import jax
import jax.numpy as jnp
from jax import lax
from jax.experimental import pallas as pl
from jax.experimental.pallas import tpu as pltpu
from jax.sharding import PartitionSpec as P

MESH = pl.DeviceIdType.MESH
F32 = jnp.float32
BF16 = jnp.bfloat16
NX = 6
LAG = 1


def dot(a, b):
    return jnp.dot(a, b, preferred_element_type=F32)


def dot_t(a, b):
    return lax.dot_general(a, b, (((0,), (0,)), ((), ())), preferred_element_type=F32)


def iota(shape, d):
    return lax.broadcasted_iota(jnp.int32, shape, d)


def onehot(cond):
    return jnp.where(cond, 1.0, 0.0).astype(BF16)


def kernel(np_, n, no, nv, a_ref, cot_ref, cvt_ref, v1_ref, v2_ref,
           a_buf, la, ww, cv_buf, t_buf, h_buf, lx, ly, l1,
           sx, sy, so, sp, rx, ry, rp, ro, px, py, qx, qy,
           a_sem, s_sem, rx_sem, ry_sem, ro_sem, p_sem, qx_sem, qy_sem):
    nd = 8
    npair = np_ // 2
    nb = nv // 8
    NY = nb - NX
    ng = n // 16
    me = lax.axis_index("dev")
    frag = lax.axis_index("frag")
    y, x, c = me // 4, (me // 2) % 2, me % 2

    def dev(k):
        dy, dx, dc = k
        return (1 - y if dy else y) * 4 + (1 - x if dx else x) * 2 + (1 - c if dc else c)

    def did(k):
        return (frag, dev(k))

    KS = [(1, 1, 0), (1, 1, 1), (1, 0, 1), (0, 1, 1), (1, 0, 0), (0, 1, 0), (0, 0, 1), (0, 0, 0)]

    def a_copy(p, g):
        slot = p % 4
        return pltpu.make_async_copy(a_ref.at[p, pl.ds(16 * g, 16)], a_buf.at[slot, pl.ds(16 * g, 16)],
                                     a_sem.at[slot])

    for p in range(2):
        for g in range(ng):
            a_copy(p, g).start()

    barrier = pltpu.get_barrier_semaphore()
    for k in KS[:-1]:
        pl.semaphore_signal(barrier, inc=1, device_id=did(k), device_id_type=MESH)

    cot = cot_ref[...]
    cvt = cvt_ref[...]
    co = dot_t(cot, onehot(iota((no, no), 0) == iota((no, no), 1))).astype(BF16)
    cv = dot_t(cvt, onehot(iota((nv, nv), 0) == iota((nv, nv), 1))).astype(BF16)
    cv_buf[...] = cv
    rep8 = onehot(iota((no * 8, no), 0) // 8 == iota((no * 8, no), 1))
    tile = onehot(iota((n, 8 * n), 0) == iota((n, 8 * n), 1) % n)
    m = dot(rep8, dot(cot, tile).astype(BF16))
    la[...] = jnp.where(iota(m.shape, 0) % 8 == iota(m.shape, 1) // n, m, 0.0).astype(BF16)
    ww[...] = jnp.zeros_like(ww)
    for par in range(2):
        for j in range(2):
            jb = iota((nv, 512), 0) + j * nv
            col = iota((nv, 512), 1)
            sel_v = onehot(col == jnp.where(jb < 128, par * 128 + jb, 256 + 48 * par + jb - 128))
            sel_o = onehot(iota((no, 512), 1) == iota((no, 512), 0) + 384 + 32 * par + no * j)
            r0 = 256 * par + 128 * j
            ww[r0:r0 + n, :] = (dot(cv, sel_v) + dot(co, sel_o)).astype(BF16)

    for p in range(2, 4):
        for g in range(ng):
            a_copy(p, g).start()

    def kron(tab, m_, kk, p_of_col, same):
        perm = onehot(iota((n, kk), 0) == p_of_col(iota((n, kk), 1)))
        r = onehot(iota((m_ * 8, m_), 0) // 8 == iota((m_ * 8, m_), 1))
        v = dot(r, dot(tab, perm).astype(BF16))
        return jnp.where(iota(v.shape, 0) % 8 == same(iota(v.shape, 1)), v, 0.0).astype(BF16)

    def send_x(i, k):
        h = (0, k[1], k[2])
        return pltpu.make_async_remote_copy(
            src_ref=sx.at[dev(k), i], dst_ref=rx.at[k[0], x * 2 + c, i],
            send_sem=s_sem.at[0], recv_sem=rx_sem.at[k[0]], device_id=did(h), device_id_type=MESH)

    def send_y(i, k):
        h = (k[0], 0, k[2])
        return pltpu.make_async_remote_copy(
            src_ref=sy.at[dev(k), i], dst_ref=ry.at[k[1], y * 2 + c, i],
            send_sem=s_sem.at[1], recv_sem=ry_sem.at[k[1]], device_id=did(h), device_id_type=MESH)

    def send_o(k):
        return pltpu.make_async_remote_copy(
            src_ref=sp.at[dev(k)], dst_ref=rp.at[me],
            send_sem=s_sem.at[2], recv_sem=ro_sem, device_id=did(k), device_id_type=MESH)

    def far_x(k):
        return bool(k[1] or k[2])

    def far_y(k):
        return bool(k[0] or k[2])

    def send_relay(i, k):
        if far_x(k) and k[0]:
            send_x(i, k).start()
        if far_y(k) and k[1]:
            send_y(i, k).start()

    def send_direct(i):
        for k in KS:
            if far_x(k) and not k[0]:
                send_x(i, k).start()
            if far_y(k) and not k[1]:
                send_y(i, k).start()

    zpad = jnp.zeros((8 * n, 128 - n), BF16)

    def pair(i, _):
        for par in range(2):
            p = 2 * i + par
            slot = p % 4

            pltpu.make_async_copy(a_ref.at[p], a_buf.at[slot], a_sem.at[slot]).wait()
            for g in range(ng):
                a0 = a_buf[slot, 16 * g:16 * g + 8].reshape(8 * n, n)
                a1 = a_buf[slot, 16 * g + 8:16 * g + 16].reshape(8 * n, n)
                w = jnp.concatenate([a0, zpad, a1, zpad], axis=1)
                t = dot(la[...], w)
                for xx in range(no):
                    tx = t[8 * xx:8 * xx + 8]
                    tx = jnp.concatenate([tx[:, 0:128], tx[:, 128:256]], axis=0).astype(BF16)
                    l0 = par * 256 + (xx % 2) * 128
                    t_buf[xx // 2, 16 * g:16 * g + 16, l0:l0 + 128] = tx

            @pl.when(p + 4 < np_)
            def _():
                for g in range(ng):
                    a_copy(p + 4, g).start()

        def step2(d, _):
            tt = t_buf[pl.ds(4 * d, 4)].reshape(4 * n, 512)
            h_buf[pl.ds(4 * d, 4)] = dot(tt, ww[...]).astype(BF16).reshape(4, n, 512)
            return 0

        lax.fori_loop(0, 2, step2, 0)

        for kn, k in enumerate(KS):
            d = dev(k)
            h = h_buf[d]
            g = dot(cvt_ref[...], h[:, 0:384]).astype(BF16).reshape(nb, 8, 384)
            if far_x(k):
                sx[d, i] = g[0:NX]
            else:
                rx[k[0], x * 2 + c, i] = g[0:NX]
            if far_y(k):
                sy[d, i] = g[NX:nb]
            else:
                ry[k[1], y * 2 + c, i] = g[NX:nb]
            so[d, i] = dot_t(h[:, 384:384 + 4 * no], cv_buf[...]).astype(BF16)
            if kn == 1:
                @pl.when(i == 0)
                def _():
                    pl.semaphore_wait(barrier, nd - 1)
            if kn > 0:
                send_relay(i, KS[kn - 1])

        @pl.when(i >= LAG)
        def _():
            send_direct(i - LAG)

        return 0

    lax.fori_loop(0, npair, pair, 0)
    for i in range(npair - LAG, npair):
        send_direct(i)

    def pack(d, _):
        sp[d, :, 0:npair * nv] = jnp.concatenate([so[d, i] for i in range(npair)], axis=1)
        return 0
    lax.fori_loop(0, nd, pack, 0)
    rp[me] = sp[me]
    for k in KS[:-1]:
        send_o(k).start()

    k4 = npair * 32
    for par in range(2):
        lx[par] = kron(cot, no, k4, lambda t: np_ * (y * 4 + t // (8 * npair)) + 2 * ((t // 8) % npair) + par,
                       lambda t: t % 8)
        ly[par] = kron(cot, no, k4, lambda t: np_ * (t // (16 * npair) * 4 + x * 2 + t // (8 * npair) % 2) + 2 * ((t // 8) % npair) + par,
                       lambda t: t % 8)

    def wait_recv(buf, sem):
        pltpu.make_async_remote_copy(
            src_ref=buf, dst_ref=buf, send_sem=s_sem.at[0], recv_sem=sem,
            device_id=did((0, 0, 1)), device_id_type=MESH).wait_recv()

    def wait_send(buf, sem):
        pltpu.make_async_remote_copy(
            src_ref=buf, dst_ref=buf, send_sem=sem, recv_sem=ro_sem,
            device_id=did((0, 0, 1)), device_id_type=MESH).wait_send()

    def wait_v2(w):
        wait_recv(rx.at[w, pl.ds(0, 3)], rx_sem.at[w])
        wait_recv(ry.at[w, pl.ds(0, 3)], ry_sem.at[w])

    def partial(r, left, w, ab):
        v = r[w, :, :, ab].reshape(k4, 384)
        main = dot(left[0], v[:, 0:128]) + dot(left[1], v[:, 128:256])
        even = dot(left[0], v[:, 256:384])
        odd = dot(left[1], v[:, 256:384])
        return main.reshape(no, 8, 128), even.reshape(no, 8, 128), odd.reshape(no, 8, 128)

    lane = iota((8, 8, 128), 2)

    def send_p(buf, out, ssem, rsem, h, ab):
        return pltpu.make_async_remote_copy(
            src_ref=buf.at[ab], dst_ref=out.at[ab], send_sem=ssem, recv_sem=rsem.at[ab],
            device_id=did(h), device_id_type=MESH)

    wait_v2(1)
    for r, left, buf, out, ssem, rsem, h, cnt in (
            (rx, lx, px, qx, p_sem.at[0], qx_sem, (1, 0, 0), NX), (ry, ly, py, qy, p_sem.at[1], qy_sem, (0, 1, 0), NY)):
        def relay(ab, _, r=r, left=left, buf=buf, out=out, ssem=ssem, rsem=rsem, h=h):
            main, even, odd = partial(r, left, 1, ab)
            buf[ab, 0:no] = main
            lo = even[0:8] + pltpu.roll(odd[0:8], 80, 2)
            hi = pltpu.roll(even[8:16], 48, 2) + odd[8:16]
            buf[ab, no:no + 8] = jnp.where(lane < 48, lo, hi)
            send_p(buf, out, ssem, rsem, h, ab).start()
            return 0
        lax.fori_loop(0, cnt, relay, 0)

    wait_v2(0)
    for r, left, cnt, base in ((rx, lx, NX, 0), (ry, ly, NY, NX)):
        def own(ab, _, r=r, left=left, base=base):
            main, even, odd = partial(r, left, 0, ab)
            rows = pl.ds(pl.multiple_of((ab + base) * 8, 8), 8)
            v2_ref[:, rows, 0:128] = main
            v2_ref[:, rows, 128:176] = (even + pltpu.roll(odd, 80, 2))[:, :, 0:48]
            return 0
        lax.fori_loop(0, cnt, own, 0)

    k8 = npair * 128
    l1[...] = kron(cvt_ref[...], nv, k8,
                   lambda t: np_ * (t // (16 * npair)) + 2 * ((t // 16) % npair) + (t // 8) % 2,
                   lambda t: t % 8)

    wait_recv(rp.at[pl.ds(0, nd - 1)], ro_sem)

    def unpack(d, _):
        v = rp[d]
        for i in range(npair):
            ro[d, i] = v[:, nv * i:nv * i + nv]
        return 0
    lax.fori_loop(0, nd, unpack, 0)

    for ib in range(4):
        def oo_rows(par):
            return ro[:, :, par * 32 + 8 * ib:par * 32 + 8 * ib + 8].reshape(npair * nd, 8, nv)
        w = jnp.concatenate([oo_rows(0), oo_rows(1)], axis=1).reshape(k8, nv)
        v1_ref[:, 8 * ib:8 * ib + 8, :] = dot(l1[...], w).reshape(nv, 8, nv)

    for buf, out, ssem, rsem, h, cnt, base in (
            (px, qx, p_sem.at[0], qx_sem, (1, 0, 0), NX, 0), (py, qy, p_sem.at[1], qy_sem, (0, 1, 0), NY, NX)):
        def add(ab, _, buf=buf, out=out, ssem=ssem, rsem=rsem, h=h, base=base):
            send_p(buf, out, ssem, rsem, h, ab).wait_recv()
            rows = pl.ds(pl.multiple_of((ab + base) * 8, 8), 8)
            v2_ref[:, rows, 0:128] += out[ab, 0:no]
            ext = out[ab, no:no + 8]
            v2_ref[0:8, rows, 128:176] += ext[:, :, 0:48]
            v2_ref[8:16, rows, 128:176] += pltpu.roll(ext, 80, 2)[:, :, 0:48]
            return 0
        lax.fori_loop(0, cnt, add, 0)

    wait_send(sx.at[pl.ds(0, 6)], s_sem.at[0])
    wait_send(sy.at[pl.ds(0, 6)], s_sem.at[1])
    wait_send(sp.at[pl.ds(0, nd - 1)], s_sem.at[2])
    wait_send(px, p_sem.at[0])
    wait_send(py, p_sem.at[1])


def solution(mesh):
    nd = mesh.shape["dev"]

    def local_part(a, co, cv):
        np_, n = a.shape[0], a.shape[1]
        no, nv = co.shape[1], cv.shape[1]
        npair, nb = np_ // 2, nv // 8
        ny = nb - NX
        lanes = -(-npair * nv // 128) * 128
        vm = pl.BlockSpec(memory_space=pltpu.VMEM)
        dma = pltpu.SemaphoreType.DMA
        v1, v2 = pl.pallas_call(
            functools.partial(kernel, np_, n, no, nv),
            out_shape=(jax.ShapeDtypeStruct((nv, no * no // nd, nv), F32),
                       jax.ShapeDtypeStruct((no, nv, no * nv // nd), F32)),
            in_specs=[pl.BlockSpec(memory_space=pl.ANY), vm, vm],
            out_specs=(vm, vm),
            scratch_shapes=[
                pltpu.VMEM((4, n, n, n), BF16),
                pltpu.VMEM((no * 8, n * 8), BF16),
                pltpu.VMEM((512, 512), BF16),
                pltpu.VMEM((n, nv), BF16),
                pltpu.VMEM((nd, n, 512), BF16),
                pltpu.VMEM((nd, n, 512), BF16),
                pltpu.VMEM((2, no * 8, npair * 32), BF16),
                pltpu.VMEM((2, no * 8, npair * 32), BF16),
                pltpu.VMEM((nv * 8, npair * 128), BF16),
                pltpu.VMEM((nd, npair, NX, 8, 384), BF16),
                pltpu.VMEM((nd, npair, ny, 8, 384), BF16),
                pltpu.VMEM((nd, npair, 4 * no, nv), BF16),
                pltpu.VMEM((nd, 4 * no, lanes), BF16),
                pltpu.VMEM((2, 4, npair, NX, 8, 384), BF16),
                pltpu.VMEM((2, 4, npair, ny, 8, 384), BF16),
                pltpu.VMEM((nd, 4 * no, lanes), BF16),
                pltpu.VMEM((nd, npair, 4 * no, nv), BF16),
                pltpu.VMEM((NX, no + 8, 8, 128), F32),
                pltpu.VMEM((ny, no + 8, 8, 128), F32),
                pltpu.VMEM((NX, no + 8, 8, 128), F32),
                pltpu.VMEM((ny, no + 8, 8, 128), F32),
                dma((4,)), dma((3,)), dma((2,)), dma((2,)), dma,
                dma((2,)), dma((NX,)), dma((ny,)),
            ],
            compiler_params=pltpu.CompilerParams(
                collective_id=0, has_side_effects=True, vmem_limit_bytes=44 * 1024 * 1024),
        )(a, co.T, cv.T)
        return v1.transpose(0, 2, 1), v2

    return jax.shard_map(local_part, mesh=mesh,
                         in_specs=(P(('frag', 'dev')), P('frag'), P('frag')),
                         out_specs=(P('frag', None, 'dev'), P('frag', None, 'dev')),
                         check_vma=False)
```

time: 74.3 us -> 57 us (0.77)
  Pallas kernels: 69.7 us -> 52.6 us
    pallas_call x1, Pallas kernels: 69.7 us -> 52.6 us  [local_part(): pl.pallas_call(functools.partial(kernel, np_, n, no, nv), out_shape=(jax....]
    unnamed x4 -> x6, local copies, waits for them, and re-layouts: 3.78 us -> 3.61 us
where the time goes in v3:
time: 57 us; the launch traced here: 56.8 us
  Pallas kernels  52.6 us (92%)
  local copies, waits for them, and re-layouts  3.61 us (6%)
  between operations  0.65 us (1%)
    pallas_call x1, Pallas kernels, local_part(): pl.pallas_call(functools.partial(kernel, np_, n, no, nv), out_shape=(jax....  52.6 us
    unnamed x6, local copies, waits for them, and re-layouts  3.61 us

profile of v3, /device:TPU:0, one launch (start us, length us, event | category | flops | bytes accessed | tf_op | source)
XLA Modules:
  0.0 56.8 jit_solution(14808977210163146463)
XLA Ops:
  0.6 0.0 copy-start
  0.6 0.7 %copy-done = bf16[112,88]{0,1:T(8,128)(2,1)S(1)} copy-done((bf16[112,88]{0,1:T(8,128)(2,1)S(1)}, bf16[112,88]{0,1:T(8,128)(2,1)}, u32[]{:S(2)}) %copy-start) | copy-done | bytes 19736
  1.4 0.0 copy-start.1
  1.4 0.7 %copy-done.1 = bf16[112,16]{0,1:T(8,128)(2,1)S(1)} copy-done((bf16[112,16]{0,1:T(8,128)(2,1)S(1)}, bf16[112,16]{0,1:T(8,128)(2,1)}, u32[]{:S(2)}) %copy-start.1) | copy-done | bytes 3608
  2.1 52.6 %shard_map.50 = (f32[88,32,88]{2,1,0:T(8,128)S(1)}, f32[16,88,176]{2,1,0:T(8,128)S(1)}) custom-call(bf16[14,112,112,112]{3,2,1,0:T(8,128)(2,1)} %a_ref.1, bf16[16,112]{1,0:T(8,128)(2,1)S(1)} %bitcast.5, bf16[88,112]{1,0:T(8,128)(2,1)S(1)} %bitcast.4), custom_call_target="tpu_custom_call" | custom-call | tf_op jit(solution)/shard_map/pallas_call | solution.py:310
  54.6 1.1 %copy.7 = f32[88,88,32]{1,2,0:T(8,128)} copy(f32[88,88,32]{1,2,0:T(8,128)S(1)} %bitcast.3) | data formatting | bytes 1982464
  55.7 1.1 %copy.8 = f32[16,88,176]{2,1,0:T(8,128)} copy(f32[16,88,176]{2,1,0:T(8,128)S(1)} %get-tuple-element.9) | data formatting | bytes 1982464
Async XLA Ops:
  0.6 0.7 %copy-start = (bf16[112,88]{0,1:T(8,128)(2,1)S(1)}, bf16[112,88]{0,1:T(8,128)(2,1)}, u32[]{:S(2)}) copy-start(bf16[112,88]{0,1:T(8,128)(2,1)} %param.5) | copy-start | bytes 59140
  1.4 0.7 %copy-start.1 = (bf16[112,16]{0,1:T(8,128)(2,1)S(1)}, bf16[112,16]{0,1:T(8,128)(2,1)}, u32[]{:S(2)}) copy-start(bf16[112,16]{0,1:T(8,128)(2,1)} %param.4) | copy-start | bytes 10756

commit v4 on v3

--- a/solution.py
+++ b/solution.py
@@ -11,7 +11,6 @@
 F32 = jnp.float32
 BF16 = jnp.bfloat16
 NX = 6
-LAG = 1
 
 
 def dot(a, b):
@@ -77,12 +76,10 @@
     ww[...] = jnp.zeros_like(ww)
     for par in range(2):
         for j in range(2):
-            jb = iota((nv, 512), 0) + j * nv
-            col = iota((nv, 512), 1)
-            sel_v = onehot(col == jnp.where(jb < 128, par * 128 + jb, 256 + 48 * par + jb - 128))
-            sel_o = onehot(iota((no, 512), 1) == iota((no, 512), 0) + 384 + 32 * par + no * j)
-            r0 = 256 * par + 128 * j
-            ww[r0:r0 + n, :] = (dot(cv, sel_v) + dot(co, sel_o)).astype(BF16)
+            jb = iota((nv, 256), 0) + j * nv
+            sel_v = onehot(iota((nv, 256), 1) == jnp.where(jb < 128, jb, jb + 32 + 48 * par))
+            sel_o = onehot(iota((no, 256), 1) == iota((no, 256), 0) + 128 + no * j)
+            ww[par, 128 * j:128 * j + n, :] = (dot(cv, sel_v) + dot(co, sel_o)).astype(BF16)
 
     for p in range(2, 4):
         for g in range(ng):
@@ -146,25 +143,22 @@
                 for xx in range(no):
                     tx = t[8 * xx:8 * xx + 8]
                     tx = jnp.concatenate([tx[:, 0:128], tx[:, 128:256]], axis=0).astype(BF16)
-                    l0 = par * 256 + (xx % 2) * 128
-                    t_buf[xx // 2, 16 * g:16 * g + 16, l0:l0 + 128] = tx
+                    l0 = (xx % 2) * 128
+                    t_buf[par, xx // 2, 16 * g:16 * g + 16, l0:l0 + 128] = tx
 
             @pl.when(p + 4 < np_)
             def _():
                 for g in range(ng):
                     a_copy(p + 4, g).start()
 
-        def step2(d, _):
-            tt = t_buf[pl.ds(4 * d, 4)].reshape(4 * n, 512)
-            h_buf[pl.ds(4 * d, 4)] = dot(tt, ww[...]).astype(BF16).reshape(4, n, 512)
-            return 0
-
-        lax.fori_loop(0, 2, step2, 0)
-
-        for kn, k in enumerate(KS):
+            h_buf[par] = dot(t_buf[par].reshape(nd * n, 256), ww[par]).astype(BF16).reshape(nd, n, 256)
+
+        for k in KS:
             d = dev(k)
-            h = h_buf[d]
-            g = dot(cvt_ref[...], h[:, 0:384]).astype(BF16).reshape(nb, 8, 384)
+            h0 = h_buf[0, d]
+            h1 = h_buf[1, d]
+            h = jnp.concatenate([h0[:, 0:128], h1[:, 0:128], h0[:, 128:256] + h1[:, 128:256]], axis=1)
+            g = dot(cvt_ref[...], h).astype(BF16).reshape(nb, 8, 384)
             if far_x(k):
                 sx[d, i] = g[0:NX]
             else:
@@ -173,24 +167,19 @@
                 sy[d, i] = g[NX:nb]
             else:
                 ry[k[1], y * 2 + c, i] = g[NX:nb]
-            so[d, i] = dot_t(h[:, 384:384 + 4 * no], cv_buf[...]).astype(BF16)
-            if kn == 1:
-                @pl.when(i == 0)
-                def _():
-                    pl.semaphore_wait(barrier, nd - 1)
-            if kn > 0:
-                send_relay(i, KS[kn - 1])
-
-        @pl.when(i >= LAG)
+            so[d, i, 0:2 * no] = dot_t(h0[:, 128:160], cv_buf[...]).astype(BF16)
+            so[d, i, 2 * no:4 * no] = dot_t(h1[:, 128:160], cv_buf[...]).astype(BF16)
+
+        @pl.when(i == 0)
         def _():
-            send_direct(i - LAG)
-
+            pl.semaphore_wait(barrier, nd - 1)
+
+        for k in KS:
+            send_relay(i, k)
+        send_direct(i)
         return 0
 
     lax.fori_loop(0, npair, pair, 0)
-    for i in range(npair - LAG, npair):
-        send_direct(i)
-
     def pack(d, _):
         sp[d, :, 0:npair * nv] = jnp.concatenate([so[d, i] for i in range(npair)], axis=1)
         return 0
@@ -227,8 +216,6 @@
         odd = dot(left[1], v[:, 256:384])
         return main.reshape(no, 8, 128), even.reshape(no, 8, 128), odd.reshape(no, 8, 128)
 
-    lane = iota((8, 8, 128), 2)
-
     def send_p(buf, out, ssem, rsem, h, ab):
         return pltpu.make_async_remote_copy(
             src_ref=buf.at[ab], dst_ref=out.at[ab], send_sem=ssem, recv_sem=rsem.at[ab],
@@ -240,9 +227,11 @@
         def relay(ab, _, r=r, left=left, buf=buf, out=out, ssem=ssem, rsem=rsem, h=h):
             main, even, odd = partial(r, left, 1, ab)
             buf[ab, 0:no] = main
-            lo = even[0:8] + pltpu.roll(odd[0:8], 80, 2)
-            hi = pltpu.roll(even[8:16], 48, 2) + odd[8:16]
-            buf[ab, no:no + 8] = jnp.where(lane < 48, lo, hi)
+            ext = (even + pltpu.roll(odd, 80, 2))[:, :, 32:80]
+            for q in range(no // 8):
+                row = jnp.concatenate([ext[8 * q + t] for t in range(8)], axis=1)
+                for t in range(3):
+                    buf[ab, no + 3 * q + t] = row[:, 128 * t:128 * t + 128]
             send_p(buf, out, ssem, rsem, h, ab).start()
             return 0
         lax.fori_loop(0, cnt, relay, 0)
@@ -253,7 +242,7 @@
             main, even, odd = partial(r, left, 0, ab)
             rows = pl.ds(pl.multiple_of((ab + base) * 8, 8), 8)
             v2_ref[:, rows, 0:128] = main
-            v2_ref[:, rows, 128:176] = (even + pltpu.roll(odd, 80, 2))[:, :, 0:48]
+            v2_ref[:, rows, 128:176] = pltpu.roll(even + pltpu.roll(odd, 80, 2), 96, 2)[:, :, 0:48]
             return 0
         lax.fori_loop(0, cnt, own, 0)
 
@@ -283,9 +272,10 @@
             send_p(buf, out, ssem, rsem, h, ab).wait_recv()
             rows = pl.ds(pl.multiple_of((ab + base) * 8, 8), 8)
             v2_ref[:, rows, 0:128] += out[ab, 0:no]
-            ext = out[ab, no:no + 8]
-            v2_ref[0:8, rows, 128:176] += ext[:, :, 0:48]
-            v2_ref[8:16, rows, 128:176] += pltpu.roll(ext, 80, 2)[:, :, 0:48]
+            for q in range(no // 8):
+                row = jnp.concatenate([out[ab, no + 3 * q + t] for t in range(3)], axis=1)
+                for t in range(8):
+                    v2_ref[8 * q + t, rows, 128:176] += row[:, 48 * t:48 * t + 48]
             return 0
         lax.fori_loop(0, cnt, add, 0)
 
@@ -316,10 +306,10 @@
             scratch_shapes=[
                 pltpu.VMEM((4, n, n, n), BF16),
                 pltpu.VMEM((no * 8, n * 8), BF16),
-                pltpu.VMEM((512, 512), BF16),
+                pltpu.VMEM((2, 256, 256), BF16),
                 pltpu.VMEM((n, nv), BF16),
-                pltpu.VMEM((nd, n, 512), BF16),
-                pltpu.VMEM((nd, n, 512), BF16),
+                pltpu.VMEM((2, nd, n, 256), BF16),
+                pltpu.VMEM((2, nd, n, 256), BF16),
                 pltpu.VMEM((2, no * 8, npair * 32), BF16),
                 pltpu.VMEM((2, no * 8, npair * 32), BF16),
                 pltpu.VMEM((nv * 8, npair * 128), BF16),
@@ -331,10 +321,10 @@
                 pltpu.VMEM((2, 4, npair, ny, 8, 384), BF16),
                 pltpu.VMEM((nd, 4 * no, lanes), BF16),
                 pltpu.VMEM((nd, npair, 4 * no, nv), BF16),
-                pltpu.VMEM((NX, no + 8, 8, 128), F32),
-                pltpu.VMEM((ny, no + 8, 8, 128), F32),
-                pltpu.VMEM((NX, no + 8, 8, 128), F32),
-                pltpu.VMEM((ny, no + 8, 8, 128), F32),
+                pltpu.VMEM((NX, no + 3 * no // 8, 8, 128), F32),
+                pltpu.VMEM((ny, no + 3 * no // 8, 8, 128), F32),
+                pltpu.VMEM((NX, no + 3 * no // 8, 8, 128), F32),
+                pltpu.VMEM((ny, no + 3 * no // 8, 8, 128), F32),
                 dma((4,)), dma((3,)), dma((2,)), dma((2,)), dma,
                 dma((2,)), dma((NX,)), dma((ny,)),
             ],

time: 57 us -> 52 us (0.912)
  Pallas kernels: 52.6 us -> 47.6 us
    pallas_call x1, Pallas kernels: 52.6 us -> 47.6 us  [local_part(): pl.pallas_call(functools.partial(kernel, np_, n, no, nv), out_shape=(jax....]
where the time goes in v4:
time: 52 us; the launch traced here: 51.8 us
  Pallas kernels  47.6 us (92%)
  local copies, waits for them, and re-layouts  3.61 us (7%)
  between operations  0.65 us (1%)
    pallas_call x1, Pallas kernels, local_part(): pl.pallas_call(functools.partial(kernel, np_, n, no, nv), out_shape=(jax....  47.6 us
    unnamed x6, local copies, waits for them, and re-layouts  3.61 us

profile of v4, /device:TPU:0, one launch (start us, length us, event | category | flops | bytes accessed | tf_op | source)
XLA Modules:
  0.0 51.8 jit_solution(921807024435935307)
XLA Ops:
  0.6 0.0 copy-start
  0.6 0.7 %copy-done = bf16[112,88]{0,1:T(8,128)(2,1)S(1)} copy-done((bf16[112,88]{0,1:T(8,128)(2,1)S(1)}, bf16[112,88]{0,1:T(8,128)(2,1)}, u32[]{:S(2)}) %copy-start) | copy-done | bytes 19736
  1.4 0.0 copy-start.1
  1.4 0.7 %copy-done.1 = bf16[112,16]{0,1:T(8,128)(2,1)S(1)} copy-done((bf16[112,16]{0,1:T(8,128)(2,1)S(1)}, bf16[112,16]{0,1:T(8,128)(2,1)}, u32[]{:S(2)}) %copy-start.1) | copy-done | bytes 3608
  2.1 47.6 %shard_map.50 = (f32[88,32,88]{2,1,0:T(8,128)S(1)}, f32[16,88,176]{2,1,0:T(8,128)S(1)}) custom-call(bf16[14,112,112,112]{3,2,1,0:T(8,128)(2,1)} %a_ref.1, bf16[16,112]{1,0:T(8,128)(2,1)S(1)} %bitcast.5, bf16[88,112]{1,0:T(8,128)(2,1)S(1)} %bitcast.4), custom_call_target="tpu_custom_call" | custom-call | tf_op jit(solution)/shard_map/pallas_call | solution.py:300
  49.6 1.1 %copy.7 = f32[88,88,32]{1,2,0:T(8,128)} copy(f32[88,88,32]{1,2,0:T(8,128)S(1)} %bitcast.3) | data formatting | bytes 1982464
  50.7 1.1 %copy.8 = f32[16,88,176]{2,1,0:T(8,128)} copy(f32[16,88,176]{2,1,0:T(8,128)S(1)} %get-tuple-element.9) | data formatting | bytes 1982464
Async XLA Ops:
  0.6 0.7 %copy-start = (bf16[112,88]{0,1:T(8,128)(2,1)S(1)}, bf16[112,88]{0,1:T(8,128)(2,1)}, u32[]{:S(2)}) copy-start(bf16[112,88]{0,1:T(8,128)(2,1)} %param.5) | copy-start | bytes 59140
  1.4 0.7 %copy-start.1 = (bf16[112,16]{0,1:T(8,128)(2,1)S(1)}, bf16[112,16]{0,1:T(8,128)(2,1)}, u32[]{:S(2)}) copy-start(bf16[112,16]{0,1:T(8,128)(2,1)} %param.4) | copy-start | bytes 10756

commit v5 on v4

v5 whole, which is shorter than its diff:
```python
import functools

import jax
import jax.numpy as jnp
from jax import lax
from jax.experimental import pallas as pl
from jax.experimental.pallas import tpu as pltpu
from jax.sharding import PartitionSpec as P

MESH = pl.DeviceIdType.MESH
F32 = jnp.float32
BF16 = jnp.bfloat16
NF = 6
EXT = 48


def dot(a, b):
    return jnp.dot(a, b, preferred_element_type=F32)


def dot_t(a, b):
    return lax.dot_general(a, b, (((0,), (0,)), ((), ())), preferred_element_type=F32)


def iota(shape, d):
    return lax.broadcasted_iota(jnp.int32, shape, d)


def onehot(cond):
    return jnp.where(cond, 1.0, 0.0).astype(BF16)


def tiles(blocks):
    return 2 * blocks + -(-2 * EXT * blocks // 128)


def kernel(np_, n, no, nv, a_ref, cot_hbm, cvt_hbm, v1_ref, v2_ref,
           cot_ref, cvt_ref, a_buf, la, ww, cv_buf, t_buf, h_buf, lf, ls, l1,
           sf, ss, so, sp, rf, rs, rp, ro, pf, ps, qf, qs,
           c_sem, a_sem, s_sem, rf_sem, rs_sem, ro_sem, p_sem, qf_sem, qs_sem):
    nd = 8
    npair = np_ // 2
    nb = nv // 8
    NS = nb - NF
    ng = n // 16
    me = lax.axis_index("dev")
    frag = lax.axis_index("frag")
    y, x, c = me // 4, (me // 2) % 2, me % 2

    def first(cd):
        return x + cd * (y - x)

    def second(cd):
        return y + cd * (x - y)

    def dev(s, f, cd, core):
        return (s + cd * (f - s)) * 4 + (f + cd * (s - f)) * 2 + core

    def flip(v, on):
        return 1 - v if on else v

    def dest(k):
        cd = flip(c, k[2])
        return dev(flip(second(cd), k[0]), flip(first(cd), k[1]), cd, cd)

    KS = [(1, 1, 0), (1, 1, 1), (1, 0, 1), (0, 1, 1), (1, 0, 0), (0, 1, 0), (0, 0, 1), (0, 0, 0)]

    def a_copy(p, g):
        slot = p % 4
        return pltpu.make_async_copy(a_ref.at[p, pl.ds(16 * g, 16)], a_buf.at[slot, pl.ds(16 * g, 16)],
                                     a_sem.at[slot])

    barrier = pltpu.get_barrier_semaphore()
    for k in KS[:-1]:
        pl.semaphore_signal(barrier, inc=1, device_id=(frag, dest(k)), device_id_type=MESH)
    coefs = [pltpu.make_async_copy(cot_hbm, cot_ref, c_sem.at[0]),
             pltpu.make_async_copy(cvt_hbm, cvt_ref, c_sem.at[1])]
    for cp in coefs:
        cp.start()
    for p in range(2):
        for g in range(ng):
            a_copy(p, g).start()
    for cp in coefs:
        cp.wait()

    cot = cot_ref[...]
    cvt = cvt_ref[...]
    co = dot_t(cot, onehot(iota((no, no), 0) == iota((no, no), 1))).astype(BF16)
    cv = dot_t(cvt, onehot(iota((nv, nv), 0) == iota((nv, nv), 1))).astype(BF16)
    cv_buf[...] = cv
    rep8 = onehot(iota((no * 8, no), 0) // 8 == iota((no * 8, no), 1))
    tile = onehot(iota((n, 8 * n), 0) == iota((n, 8 * n), 1) % n)
    m = dot(rep8, dot(cot, tile).astype(BF16))
    la[...] = jnp.where(iota(m.shape, 0) % 8 == iota(m.shape, 1) // n, m, 0.0).astype(BF16)
    ww[...] = jnp.zeros_like(ww)
    for par in range(2):
        for j in range(2):
            jb = iota((nv, 256), 0) + j * nv
            sel_v = onehot(iota((nv, 256), 1) == jnp.where(jb < 128, jb, jb + 32 + EXT * par))
            sel_o = onehot(iota((no, 256), 1) == iota((no, 256), 0) + 128 + no * j)
            ww[par, 128 * j:128 * j + n, :] = (dot(cv, sel_v) + dot(co, sel_o)).astype(BF16)

    for p in range(2, 4):
        for g in range(ng):
            a_copy(p, g).start()

    def send_f(i, k):
        cd = flip(c, k[2])
        return pltpu.make_async_remote_copy(
            src_ref=sf.at[dest(k), i], dst_ref=rf.at[k[0], first(cd) * 2 + c, i],
            send_sem=s_sem.at[0], recv_sem=rf_sem.at[k[0]],
            device_id=(frag, dev(second(cd), flip(first(cd), k[1]), cd, cd)), device_id_type=MESH)

    def send_s(i, k):
        cd = flip(c, k[2])
        return pltpu.make_async_remote_copy(
            src_ref=ss.at[dest(k), i], dst_ref=rs.at[k[1], second(cd) * 2 + c, i],
            send_sem=s_sem.at[1], recv_sem=rs_sem.at[k[1]],
            device_id=(frag, dev(flip(second(cd), k[0]), first(cd), cd, cd)), device_id_type=MESH)

    def send_o(k):
        return pltpu.make_async_remote_copy(
            src_ref=sp.at[dest(k)], dst_ref=rp.at[me],
            send_sem=s_sem.at[2], recv_sem=ro_sem, device_id=(frag, dest(k)), device_id_type=MESH)

    def far_f(k):
        return bool(k[1] or k[2])

    def far_s(k):
        return bool(k[0] or k[2])

    lane = iota((8, 128), 1)

    def put(buf, idx, g, blocks):
        for t, b in enumerate(blocks):
            for par in range(2):
                buf[idx + (2 * t + par,)] = g[8 * b:8 * b + 8, 128 * par:128 * par + 128].astype(BF16)
        rolled = []
        for t, b in enumerate(blocks):
            sh = (2 * EXT * t - 32) % 128
            rolled.append(pltpu.roll(g[8 * b:8 * b + 8, 256:384], sh, 1))
        nt = len(blocks)
        for u in range(tiles(nt) - 2 * nt):
            parts = [t for t in range(nt) if 96 * t < 128 * u + 128 and 96 * t + 96 > 128 * u]
            v = rolled[parts[0]]
            for t in parts[1:]:
                v = jnp.where(lane < 96 * t - 128 * u, v, rolled[t])
            buf[idx + (2 * nt + u,)] = v.astype(BF16)

    zpad = jnp.zeros((8 * n, 128 - n), BF16)

    def pair(i, _):
        for par in range(2):
            p = 2 * i + par
            slot = p % 4
            pltpu.make_async_copy(a_ref.at[p], a_buf.at[slot], a_sem.at[slot]).wait()
            for g in range(ng):
                a0 = a_buf[slot, 16 * g:16 * g + 8].reshape(8 * n, n)
                a1 = a_buf[slot, 16 * g + 8:16 * g + 16].reshape(8 * n, n)
                w = jnp.concatenate([a0, zpad, a1, zpad], axis=1)
                t = dot(la[...], w)
                for xx in range(no):
                    tx = t[8 * xx:8 * xx + 8]
                    tx = jnp.concatenate([tx[:, 0:128], tx[:, 128:256]], axis=0).astype(BF16)
                    l0 = (xx % 2) * 128
                    t_buf[par, xx // 2, 16 * g:16 * g + 16, l0:l0 + 128] = tx

            @pl.when(p + 4 < np_)
            def _():
                for g in range(ng):
                    a_copy(p + 4, g).start()

            h_buf[par] = dot(t_buf[par].reshape(nd * n, 256), ww[par]).astype(BF16).reshape(nd, n, 256)

        for k in KS:
            d = dest(k)
            cd = flip(c, k[2])
            h0 = h_buf[0, d]
            h1 = h_buf[1, d]
            h = jnp.concatenate([h0[:, 0:128], h1[:, 0:128], h0[:, 128:256] + h1[:, 128:256]], axis=1)
            g = dot(cvt_ref[...], h)
            if far_f(k):
                put(sf, (d, i), g, range(NF))
            else:
                put(rf, (k[0], first(cd) * 2 + c, i), g, range(NF))
            if far_s(k):
                put(ss, (d, i), g, range(NF, nb))
            else:
                put(rs, (k[1], second(cd) * 2 + c, i), g, range(NF, nb))
            so[d, i, 0:2 * no] = dot_t(h0[:, 128:160], cv_buf[...]).astype(BF16)
            so[d, i, 2 * no:4 * no] = dot_t(h1[:, 128:160], cv_buf[...]).astype(BF16)

        @pl.when(i == 0)
        def _():
            pl.semaphore_wait(barrier, nd - 1)

        for relayed in (1, 0):
            for k in KS:
                if far_f(k) and k[0] == relayed:
                    send_f(i, k).start()
                if far_s(k) and k[1] == relayed:
                    send_s(i, k).start()
        return 0

    lax.fori_loop(0, npair, pair, 0)

    def pack(d, _):
        sp[d, :, 0:npair * nv] = jnp.concatenate([so[d, i] for i in range(npair)], axis=1)
        return 0
    lax.fori_loop(0, nd, pack, 0)
    rp[me] = sp[me]
    for k in KS[:-1]:
        send_o(k).start()

    def kron(tab, m_, kk, p_of_col):
        perm = onehot(iota((n, kk), 0) == p_of_col(iota((n, kk), 1)))
        r = onehot(iota((m_ * 8, m_), 0) // 8 == iota((m_ * 8, m_), 1))
        v = dot(r, dot(tab, perm).astype(BF16))
        return jnp.where(iota(v.shape, 0) % 8 == iota(v.shape, 1) % 8, v, 0.0).astype(BF16)

    k4 = npair * 32
    for par in range(2):
        def p_f(t):
            src = t // (8 * npair)
            return np_ * dev(second(c), src // 2, c, src % 2) + 2 * ((t // 8) % npair) + par

        def p_s(t):
            src = t // (8 * npair)
            return np_ * dev(src // 2, first(c), c, src % 2) + 2 * ((t // 8) % npair) + par

        lf[par] = kron(cot_ref[...], no, k4, p_f)
        ls[par] = kron(cot_ref[...], no, k4, p_s)

    def wait_recv(buf, sem):
        pltpu.make_async_remote_copy(
            src_ref=buf, dst_ref=buf, send_sem=s_sem.at[0], recv_sem=sem,
            device_id=(frag, dest((0, 0, 1))), device_id_type=MESH).wait_recv()

    def wait_send(buf, sem):
        pltpu.make_async_remote_copy(
            src_ref=buf, dst_ref=buf, send_sem=sem, recv_sem=ro_sem,
            device_id=(frag, dest((0, 0, 1))), device_id_type=MESH).wait_send()

    lane_k = iota((k4, 128), 1)

    def partial(r, left, w, t, nt):
        def rows(u):
            return r[w, :, :, u].reshape(k4, 128)
        u, off = 96 * t // 128, 96 * t % 128
        e = rows(2 * nt + u)
        if off + 96 > 128:
            e = jnp.where(lane_k >= off, e, rows(2 * nt + u + 1))
        r0 = dot(left[0], jnp.concatenate([rows(2 * t), e], axis=1))
        r1 = dot(left[1], jnp.concatenate([rows(2 * t + 1), e], axis=1))
        main = r0[:, 0:128] + r1[:, 0:128]
        ext = r0[:, 128:256] + pltpu.roll(r1[:, 128:256], 128 - EXT, 1)
        if off:
            ext = pltpu.roll(ext, 128 - off, 1)
        return main.reshape(no, 8, 128), ext.reshape(no, 8, 128)

    def send_p(buf, out, ssem, rsem, h, t):
        return pltpu.make_async_remote_copy(
            src_ref=buf.at[t], dst_ref=out.at[t], send_sem=ssem, recv_sem=rsem.at[t],
            device_id=(frag, dest(h)), device_id_type=MESH)

    F = (rf, lf, pf, qf, p_sem.at[0], qf_sem, (1, 0, 0), NF, 0)
    S = (rs, ls, ps, qs, p_sem.at[1], qs_sem, (0, 1, 0), NS, NF)
    order = [(q, t) for t in range(NF) for q in (F, S) if t < q[7]]

    wait_recv(rf.at[1, pl.ds(0, 3)], rf_sem.at[1])
    wait_recv(rs.at[1, pl.ds(0, 3)], rs_sem.at[1])
    for (r, left, buf, out, ssem, rsem, h, nt, _), t in order:
        main, ext = partial(r, left, 1, t, nt)
        buf[t, 0:no] = main
        for q in range(no // 8):
            row = jnp.concatenate([ext[8 * q + v][:, 0:EXT] for v in range(8)], axis=1)
            for v in range(3):
                buf[t, no + 3 * q + v] = row[:, 128 * v:128 * v + 128]
        send_p(buf, out, ssem, rsem, h, t).start()

    wait_recv(rf.at[0, pl.ds(0, 3)], rf_sem.at[0])
    wait_recv(rs.at[0, pl.ds(0, 3)], rs_sem.at[0])
    for (r, left, _, _, _, _, _, nt, base), t in order:
        main, ext = partial(r, left, 0, t, nt)
        r0 = 8 * (base + t)
        v2_ref[:, r0:r0 + 8, 0:128] = main
        v2_ref[:, r0:r0 + 8, 128:128 + EXT] = ext[:, :, 0:EXT]

    k8 = npair * 128
    l1[...] = kron(cvt_ref[...], nv, k8,
                   lambda t: np_ * (t // (16 * npair)) + 2 * ((t // 16) % npair) + (t // 8) % 2)

    wait_recv(rp.at[pl.ds(0, nd - 1)], ro_sem)

    def unpack(d, _):
        v = rp[d]
        for i in range(npair):
            ro[d, i] = v[:, nv * i:nv * i + nv]
        return 0
    lax.fori_loop(0, nd, unpack, 0)

    for ib in range(4):
        def oo_rows(par):
            return ro[:, :, par * 32 + 8 * ib:par * 32 + 8 * ib + 8].reshape(npair * nd, 8, nv)
        w = jnp.concatenate([oo_rows(0), oo_rows(1)], axis=1).reshape(k8, nv)
        v1_ref[:, 8 * ib:8 * ib + 8, :] = dot(l1[...], w).reshape(nv, 8, nv)

    for (_, _, buf, out, ssem, rsem, h, nt, base), t in order:
        send_p(buf, out, ssem, rsem, h, t).wait_recv()
        r0 = 8 * (base + t)
        v2_ref[:, r0:r0 + 8, 0:128] += out[t, 0:no]
        for q in range(no // 8):
            row = jnp.concatenate([out[t, no + 3 * q + v] for v in range(3)], axis=1)
            for v in range(8):
                v2_ref[8 * q + v, r0:r0 + 8, 128:128 + EXT] += row[:, EXT * v:EXT * v + EXT]

    wait_send(sf.at[pl.ds(0, 6)], s_sem.at[0])
    wait_send(ss.at[pl.ds(0, 6)], s_sem.at[1])
    wait_send(sp.at[pl.ds(0, nd - 1)], s_sem.at[2])
    wait_send(pf, p_sem.at[0])
    wait_send(ps, p_sem.at[1])


def solution(mesh):
    nd = mesh.shape["dev"]

    def local_part(a, co, cv):
        np_, n = a.shape[0], a.shape[1]
        no, nv = co.shape[1], cv.shape[1]
        npair, nb = np_ // 2, nv // 8
        ns = nb - NF
        lanes = -(-npair * nv // 128) * 128
        vm = pl.BlockSpec(memory_space=pltpu.VMEM)
        hbm = pl.BlockSpec(memory_space=pltpu.HBM)
        dma = pltpu.SemaphoreType.DMA
        v1, v2 = pl.pallas_call(
            functools.partial(kernel, np_, n, no, nv),
            out_shape=(jax.ShapeDtypeStruct((nv, no * no // nd, nv), F32),
                       jax.ShapeDtypeStruct((no, nv, no * nv // nd), F32)),
            in_specs=[hbm, hbm, hbm],
            out_specs=(vm, vm),
            scratch_shapes=[
                pltpu.VMEM((no, n), BF16),
                pltpu.VMEM((nv, n), BF16),
                pltpu.VMEM((4, n, n, n), BF16),
                pltpu.VMEM((no * 8, n * 8), BF16),
                pltpu.VMEM((2, 256, 256), BF16),
                pltpu.VMEM((n, nv), BF16),
                pltpu.VMEM((2, nd, n, 256), BF16),
                pltpu.VMEM((2, nd, n, 256), BF16),
                pltpu.VMEM((2, no * 8, npair * 32), BF16),
                pltpu.VMEM((2, no * 8, npair * 32), BF16),
                pltpu.VMEM((nv * 8, npair * 128), BF16),
                pltpu.VMEM((nd, npair, tiles(NF), 8, 128), BF16),
                pltpu.VMEM((nd, npair, tiles(ns), 8, 128), BF16),
                pltpu.VMEM((nd, npair, 4 * no, nv), BF16),
                pltpu.VMEM((nd, 4 * no, lanes), BF16),
                pltpu.VMEM((2, 4, npair, tiles(NF), 8, 128), BF16),
                pltpu.VMEM((2, 4, npair, tiles(ns), 8, 128), BF16),
                pltpu.VMEM((nd, 4 * no, lanes), BF16),
                pltpu.VMEM((nd, npair, 4 * no, nv), BF16),
                pltpu.VMEM((NF, no + 3 * no // 8, 8, 128), F32),
                pltpu.VMEM((ns, no + 3 * no // 8, 8, 128), F32),
                pltpu.VMEM((NF, no + 3 * no // 8, 8, 128), F32),
                pltpu.VMEM((ns, no + 3 * no // 8, 8, 128), F32),
                dma((2,)), dma((4,)), dma((3,)), dma((2,)), dma((2,)), dma,
                dma((2,)), dma((NF,)), dma((ns,)),
            ],
            compiler_params=pltpu.CompilerParams(
                collective_id=0, has_side_effects=True, vmem_limit_bytes=44 * 1024 * 1024),
        )(a, co.T, cv.T)
        return v1.transpose(0, 2, 1), v2

    return jax.shard_map(local_part, mesh=mesh,
                         in_specs=(P(('frag', 'dev')), P('frag'), P('frag')),
                         out_specs=(P('frag', None, 'dev'), P('frag', None, 'dev')),
                         check_vma=False)
```

time: 52 us -> 50.3 us (0.967)
  Pallas kernels: 47.6 us -> 45.9 us
    pallas_call x1, Pallas kernels: 47.6 us -> 45.9 us  [local_part(): pl.pallas_call(functools.partial(kernel, np_, n, no, nv), out_shape=(jax....]
where the time goes in v5:
time: 50.3 us; the launch traced here: 50.1 us
  Pallas kernels  45.9 us (91%)
  local copies, waits for them, and re-layouts  3.61 us (7%)
  between operations  0.65 us (1%)
    pallas_call x1, Pallas kernels, local_part(): pl.pallas_call(functools.partial(kernel, np_, n, no, nv), out_shape=(jax....  45.9 us
    unnamed x6, local copies, waits for them, and re-layouts  3.61 us

profile of v5, /device:TPU:0, one launch (start us, length us, event | category | flops | bytes accessed | tf_op | source)
XLA Modules:
  0.0 50.1 jit_solution(1682364263482689797)
XLA Ops:
  0.6 0.0 copy-start
  0.6 0.7 %copy-done = bf16[112,88]{0,1:T(8,128)(2,1)S(1)} copy-done((bf16[112,88]{0,1:T(8,128)(2,1)S(1)}, bf16[112,88]{0,1:T(8,128)(2,1)}, u32[]{:S(2)}) %copy-start) | copy-done | bytes 19736
  1.4 0.0 copy-start.1
  1.4 0.7 %copy-done.1 = bf16[112,16]{0,1:T(8,128)(2,1)S(1)} copy-done((bf16[112,16]{0,1:T(8,128)(2,1)S(1)}, bf16[112,16]{0,1:T(8,128)(2,1)}, u32[]{:S(2)}) %copy-start.1) | copy-done | bytes 3608
  2.1 45.9 %shard_map.50 = (f32[88,32,88]{2,1,0:T(8,128)S(1)}, f32[16,88,176]{2,1,0:T(8,128)S(1)}) custom-call(bf16[14,112,112,112]{3,2,1,0:T(8,128)(2,1)} %a_ref.1, bf16[16,112]{1,0:T(8,128)(2,1)S(1)} %bitcast.5, bf16[88,112]{1,0:T(8,128)(2,1)S(1)} %bitcast.4), custom_call_target="tpu_custom_call" | custom-call | tf_op jit(solution)/shard_map/pallas_call | solution.py:336
  47.9 1.1 %copy.7 = f32[88,88,32]{1,2,0:T(8,128)} copy(f32[88,88,32]{1,2,0:T(8,128)S(1)} %bitcast.3) | data formatting | bytes 1982464
  49.0 1.1 %copy.8 = f32[16,88,176]{2,1,0:T(8,128)} copy(f32[16,88,176]{2,1,0:T(8,128)S(1)} %get-tuple-element.9) | data formatting | bytes 1982464
Async XLA Ops:
  0.6 0.7 %copy-start = (bf16[112,88]{0,1:T(8,128)(2,1)S(1)}, bf16[112,88]{0,1:T(8,128)(2,1)}, u32[]{:S(2)}) copy-start(bf16[112,88]{0,1:T(8,128)(2,1)} %param.5) | copy-start | bytes 59140
  1.4 0.7 %copy-start.1 = (bf16[112,16]{0,1:T(8,128)(2,1)S(1)}, bf16[112,16]{0,1:T(8,128)(2,1)}, u32[]{:S(2)}) copy-start(bf16[112,16]{0,1:T(8,128)(2,1)} %param.4) | copy-start | bytes 10756

commit v6 on v5

--- a/solution.py
+++ b/solution.py
@@ -35,9 +35,9 @@
 
 
 def kernel(np_, n, no, nv, a_ref, cot_hbm, cvt_hbm, v1_ref, v2_ref,
-           cot_ref, cvt_ref, a_buf, la, ww, cv_buf, t_buf, h_buf, lf, ls, l1,
-           sf, ss, so, sp, rf, rs, rp, ro, pf, ps, qf, qs,
-           c_sem, a_sem, s_sem, rf_sem, rs_sem, ro_sem, p_sem, qf_sem, qs_sem):
+           cot_ref, cvt_ref, a_buf, la, ww, cvs, t_buf, h_buf, lf, ls, l1,
+           sf, ss, sp, rf, rs, rp, ro, pf, ps, qf, qs,
+           c_sem, a_sem, s_sem, rf_sem, rs_sem, ro_sem, p_sem, qf_sem, qs_sem, d_sem):
     nd = 8
     npair = np_ // 2
     nb = nv // 8
@@ -64,6 +64,7 @@
         return dev(flip(second(cd), k[0]), flip(first(cd), k[1]), cd, cd)
 
     KS = [(1, 1, 0), (1, 1, 1), (1, 0, 1), (0, 1, 1), (1, 0, 0), (0, 1, 0), (0, 0, 1), (0, 0, 0)]
+    NEAR = [k for k in KS[:-1] if not (k[0] and k[1])]
 
     def a_copy(p, g):
         slot = p % 4
@@ -71,15 +72,14 @@
                                      a_sem.at[slot])
 
     barrier = pltpu.get_barrier_semaphore()
-    for k in KS[:-1]:
+    for k in NEAR:
         pl.semaphore_signal(barrier, inc=1, device_id=(frag, dest(k)), device_id_type=MESH)
     coefs = [pltpu.make_async_copy(cot_hbm, cot_ref, c_sem.at[0]),
              pltpu.make_async_copy(cvt_hbm, cvt_ref, c_sem.at[1])]
     for cp in coefs:
         cp.start()
-    for p in range(2):
-        for g in range(ng):
-            a_copy(p, g).start()
+    for g in range(ng):
+        a_copy(0, g).start()
     for cp in coefs:
         cp.wait()
 
@@ -87,40 +87,46 @@
     cvt = cvt_ref[...]
     co = dot_t(cot, onehot(iota((no, no), 0) == iota((no, no), 1))).astype(BF16)
     cv = dot_t(cvt, onehot(iota((nv, nv), 0) == iota((nv, nv), 1))).astype(BF16)
-    cv_buf[...] = cv
     rep8 = onehot(iota((no * 8, no), 0) // 8 == iota((no * 8, no), 1))
     tile = onehot(iota((n, 8 * n), 0) == iota((n, 8 * n), 1) % n)
     m = dot(rep8, dot(cot, tile).astype(BF16))
     la[...] = jnp.where(iota(m.shape, 0) % 8 == iota(m.shape, 1) // n, m, 0.0).astype(BF16)
+    for g in range(ng):
+        a_copy(1, g).start()
     ww[...] = jnp.zeros_like(ww)
     for par in range(2):
         for j in range(2):
             jb = iota((nv, 256), 0) + j * nv
             sel_v = onehot(iota((nv, 256), 1) == jnp.where(jb < 128, jb, jb + 32 + EXT * par))
-            sel_o = onehot(iota((no, 256), 1) == iota((no, 256), 0) + 128 + no * j)
+            sel_o = onehot(iota((no, 256), 1) == iota((no, 256), 0) + 128 + 32 * par + no * j)
             ww[par, 128 * j:128 * j + n, :] = (dot(cv, sel_v) + dot(co, sel_o)).astype(BF16)
 
     for p in range(2, 4):
         for g in range(ng):
             a_copy(p, g).start()
 
-    def send_f(i, k):
+    def span(part, nt):
+        return {None: pl.ds(0, tiles(nt)), 0: pl.ds(0, nt), 1: pl.ds(nt, tiles(nt) - nt)}[part]
+
+    def send_f(i, k, part=None):
         cd = flip(c, k[2])
+        part = span(part, NF)
         return pltpu.make_async_remote_copy(
-            src_ref=sf.at[dest(k), i], dst_ref=rf.at[k[0], first(cd) * 2 + c, i],
+            src_ref=sf.at[dest(k), i, part], dst_ref=rf.at[k[0], first(cd) * 2 + c, i, part],
             send_sem=s_sem.at[0], recv_sem=rf_sem.at[k[0]],
             device_id=(frag, dev(second(cd), flip(first(cd), k[1]), cd, cd)), device_id_type=MESH)
 
-    def send_s(i, k):
+    def send_s(i, k, part=None):
         cd = flip(c, k[2])
+        part = span(part, NS)
         return pltpu.make_async_remote_copy(
-            src_ref=ss.at[dest(k), i], dst_ref=rs.at[k[1], second(cd) * 2 + c, i],
+            src_ref=ss.at[dest(k), i, part], dst_ref=rs.at[k[1], second(cd) * 2 + c, i, part],
             send_sem=s_sem.at[1], recv_sem=rs_sem.at[k[1]],
             device_id=(frag, dev(flip(second(cd), k[0]), first(cd), cd, cd)), device_id_type=MESH)
 
     def send_o(k):
         return pltpu.make_async_remote_copy(
-            src_ref=sp.at[dest(k)], dst_ref=rp.at[me],
+            src_ref=sp.at[dest(k), pl.ds(0, rp.shape[1])], dst_ref=rp.at[me],
             send_sem=s_sem.at[2], recv_sem=ro_sem, device_id=(frag, dest(k)), device_id_type=MESH)
 
     def far_f(k):
@@ -131,14 +137,14 @@
 
     lane = iota((8, 128), 1)
 
-    def put(buf, idx, g, blocks):
+    def put_row(buf, idx, par, g, blocks):
         for t, b in enumerate(blocks):
-            for par in range(2):
-                buf[idx + (2 * t + par,)] = g[8 * b:8 * b + 8, 128 * par:128 * par + 128].astype(BF16)
+            buf[idx + (len(blocks) * par + t,)] = g[8 * b:8 * b + 8].astype(BF16)
+
+    def put_ext(buf, idx, g, blocks):
         rolled = []
         for t, b in enumerate(blocks):
-            sh = (2 * EXT * t - 32) % 128
-            rolled.append(pltpu.roll(g[8 * b:8 * b + 8, 256:384], sh, 1))
+            rolled.append(pltpu.roll(g[8 * b:8 * b + 8], (2 * EXT * t - 32) % 128, 1))
         nt = len(blocks)
         for u in range(tiles(nt) - 2 * nt):
             parts = [t for t in range(nt) if 96 * t < 128 * u + 128 and 96 * t + 96 > 128 * u]
@@ -147,68 +153,99 @@
                 v = jnp.where(lane < 96 * t - 128 * u, v, rolled[t])
             buf[idx + (2 * nt + u,)] = v.astype(BF16)
 
+    def places(i, k):
+        d = dest(k)
+        cd = flip(c, k[2])
+        return ((sf, (d, i), range(NF)) if far_f(k) else (rf, (k[0], first(cd) * 2 + c, i), range(NF)),
+                (ss, (d, i), range(NF, nb)) if far_s(k) else (rs, (k[1], second(cd) * 2 + c, i), range(NF, nb)))
+
     zpad = jnp.zeros((8 * n, 128 - n), BF16)
-
-    def pair(i, _):
-        for par in range(2):
-            p = 2 * i + par
-            slot = p % 4
-            pltpu.make_async_copy(a_ref.at[p], a_buf.at[slot], a_sem.at[slot]).wait()
-            for g in range(ng):
-                a0 = a_buf[slot, 16 * g:16 * g + 8].reshape(8 * n, n)
-                a1 = a_buf[slot, 16 * g + 8:16 * g + 16].reshape(8 * n, n)
-                w = jnp.concatenate([a0, zpad, a1, zpad], axis=1)
-                t = dot(la[...], w)
-                for xx in range(no):
-                    tx = t[8 * xx:8 * xx + 8]
-                    tx = jnp.concatenate([tx[:, 0:128], tx[:, 128:256]], axis=0).astype(BF16)
-                    l0 = (xx % 2) * 128
-                    t_buf[par, xx // 2, 16 * g:16 * g + 16, l0:l0 + 128] = tx
-
-            @pl.when(p + 4 < np_)
-            def _():
-                for g in range(ng):
-                    a_copy(p + 4, g).start()
-
-            h_buf[par] = dot(t_buf[par].reshape(nd * n, 256), ww[par]).astype(BF16).reshape(nd, n, 256)
-
+    lane_n = iota((n, 128), 1)
+
+    def wait_row(p):
+        pltpu.make_async_copy(a_ref.at[p], a_buf.at[p % 4], a_sem.at[p % 4]).wait()
+
+    def steps12(p, par):
+        slot = p % 4
+        for g in range(ng):
+            a0 = a_buf[slot, 16 * g:16 * g + 8].reshape(8 * n, n)
+            a1 = a_buf[slot, 16 * g + 8:16 * g + 16].reshape(8 * n, n)
+            w = jnp.concatenate([a0, zpad, a1, zpad], axis=1)
+            t = dot(la[...], w)
+            for xx in range(no):
+                tx = t[8 * xx:8 * xx + 8]
+                tx = jnp.concatenate([tx[:, 0:128], tx[:, 128:256]], axis=0).astype(BF16)
+                l0 = (xx % 2) * 128
+                t_buf[par, xx // 2, 16 * g:16 * g + 16, l0:l0 + 128] = tx
+        for e in range(0, nd, 4):
+            hh = dot(t_buf[par, e:e + 4].reshape(4 * n, 256), ww[par])
+            h_buf[par, e:e + 4] = hh.astype(BF16).reshape(4, n, 256)
+
+    def step3(i, rows):
         for k in KS:
             d = dest(k)
-            cd = flip(c, k[2])
-            h0 = h_buf[0, d]
-            h1 = h_buf[1, d]
-            h = jnp.concatenate([h0[:, 0:128], h1[:, 0:128], h0[:, 128:256] + h1[:, 128:256]], axis=1)
-            g = dot(cvt_ref[...], h)
-            if far_f(k):
-                put(sf, (d, i), g, range(NF))
-            else:
-                put(rf, (k[0], first(cd) * 2 + c, i), g, range(NF))
-            if far_s(k):
-                put(ss, (d, i), g, range(NF, nb))
-            else:
-                put(rs, (k[1], second(cd) * 2 + c, i), g, range(NF, nb))
-            so[d, i, 0:2 * no] = dot_t(h0[:, 128:160], cv_buf[...]).astype(BF16)
-            so[d, i, 2 * no:4 * no] = dot_t(h1[:, 128:160], cv_buf[...]).astype(BF16)
-
-        @pl.when(i == 0)
-        def _():
-            pl.semaphore_wait(barrier, nd - 1)
-
+            hs = [h_buf[0, d], h_buf[1, d]]
+            e0, e1 = hs[0][:, 128:256], hs[1][:, 128:256]
+            cols = [hs[par][:, 0:128] for par in rows]
+            if 1 in rows:
+                cols.append(jnp.where(lane_n < 80, e0, e1))
+            g = dot(cvt_ref[...], jnp.concatenate(cols, axis=1) if len(cols) > 1 else cols[0])
+            for buf, idx, blocks in places(i, k):
+                for q, par in enumerate(rows):
+                    put_row(buf, idx, par, g[:, 128 * q:128 * q + 128], blocks)
+                if 1 in rows:
+                    put_ext(buf, idx, g[:, 128 * len(rows):], blocks)
+            if 1 in rows:
+                go = dot_t(jnp.where(lane_n < 32, e0, e1)[:, 0:64], cvs[i]).astype(BF16)
+                for u in range(2):
+                    sp[d, nv * i // 128 + u] += go[:, 128 * u:128 * u + 128]
+
+    def sends(i, part=None):
         for relayed in (1, 0):
             for k in KS:
                 if far_f(k) and k[0] == relayed:
-                    send_f(i, k).start()
+                    send_f(i, k, part).start()
                 if far_s(k) and k[1] == relayed:
-                    send_s(i, k).start()
+                    send_s(i, k, part).start()
+
+    def pair(i, _):
+        wait_row(2 * i)
+        wait_row(2 * i + 1)
+        steps12(2 * i, 0)
+        steps12(2 * i + 1, 1)
+        step3(i, (0, 1))
+
+        @pl.when(2 * i + 4 < np_)
+        def _():
+            for p in (2 * i + 4, 2 * i + 5):
+                for g in range(ng):
+                    a_copy(p, g).start()
+
+        sends(i)
         return 0
 
-    lax.fori_loop(0, npair, pair, 0)
-
-    def pack(d, _):
-        sp[d, :, 0:npair * nv] = jnp.concatenate([so[d, i] for i in range(npair)], axis=1)
-        return 0
-    lax.fori_loop(0, nd, pack, 0)
-    rp[me] = sp[me]
+    wait_row(0)
+    steps12(0, 0)
+    step3(0, (0,))
+    pl.semaphore_wait(barrier, len(NEAR))
+    sends(0, 0)
+    pl.semaphore_signal(d_sem, inc=1, device_id=(frag, dest((0, 1, 0))), device_id_type=MESH)
+    sp[...] = jnp.zeros_like(sp)
+    for i in range(npair):
+        cvs[i] = dot(cv, onehot(iota((nv, 256), 1) == iota((nv, 256), 0) + nv * i % 128)).astype(BF16)
+    wait_row(1)
+    steps12(1, 1)
+    step3(0, (1,))
+    for p in (4, 5):
+        for g in range(ng):
+            a_copy(p, g).start()
+    sends(0, 1)
+
+    lax.fori_loop(1, npair, pair, 0)
+
+    pl.semaphore_wait(d_sem, 1)
+    nt = rp.shape[1]
+    rp[me] = sp[me, 0:nt]
     for k in KS[:-1]:
         send_o(k).start()
 
@@ -250,8 +287,8 @@
         e = rows(2 * nt + u)
         if off + 96 > 128:
             e = jnp.where(lane_k >= off, e, rows(2 * nt + u + 1))
-        r0 = dot(left[0], jnp.concatenate([rows(2 * t), e], axis=1))
-        r1 = dot(left[1], jnp.concatenate([rows(2 * t + 1), e], axis=1))
+        r0 = dot(left[0], jnp.concatenate([rows(t), e], axis=1))
+        r1 = dot(left[1], jnp.concatenate([rows(nt + t), e], axis=1))
         main = r0[:, 0:128] + r1[:, 0:128]
         ext = r0[:, 128:256] + pltpu.roll(r1[:, 128:256], 128 - EXT, 1)
         if off:
@@ -293,7 +330,7 @@
     wait_recv(rp.at[pl.ds(0, nd - 1)], ro_sem)
 
     def unpack(d, _):
-        v = rp[d]
+        v = jnp.concatenate([rp[d, u] for u in range(rp.shape[1])], axis=1)
         for i in range(npair):
             ro[d, i] = v[:, nv * i:nv * i + nv]
         return 0
@@ -316,7 +353,7 @@
 
     wait_send(sf.at[pl.ds(0, 6)], s_sem.at[0])
     wait_send(ss.at[pl.ds(0, 6)], s_sem.at[1])
-    wait_send(sp.at[pl.ds(0, nd - 1)], s_sem.at[2])
+    wait_send(rp.at[pl.ds(0, nd - 1)], s_sem.at[2])
     wait_send(pf, p_sem.at[0])
     wait_send(ps, p_sem.at[1])
 
@@ -329,7 +366,7 @@
         no, nv = co.shape[1], cv.shape[1]
         npair, nb = np_ // 2, nv // 8
         ns = nb - NF
-        lanes = -(-npair * nv // 128) * 128
+        lanes = -(-npair * nv // 128)
         vm = pl.BlockSpec(memory_space=pltpu.VMEM)
         hbm = pl.BlockSpec(memory_space=pltpu.HBM)
         dma = pltpu.SemaphoreType.DMA
@@ -345,7 +382,7 @@
                 pltpu.VMEM((4, n, n, n), BF16),
                 pltpu.VMEM((no * 8, n * 8), BF16),
                 pltpu.VMEM((2, 256, 256), BF16),
-                pltpu.VMEM((n, nv), BF16),
+                pltpu.VMEM((npair, n, 256), BF16),
                 pltpu.VMEM((2, nd, n, 256), BF16),
                 pltpu.VMEM((2, nd, n, 256), BF16),
                 pltpu.VMEM((2, no * 8, npair * 32), BF16),
@@ -353,22 +390,21 @@
                 pltpu.VMEM((nv * 8, npair * 128), BF16),
                 pltpu.VMEM((nd, npair, tiles(NF), 8, 128), BF16),
                 pltpu.VMEM((nd, npair, tiles(ns), 8, 128), BF16),
-                pltpu.VMEM((nd, npair, 4 * no, nv), BF16),
-                pltpu.VMEM((nd, 4 * no, lanes), BF16),
+                pltpu.VMEM((nd, lanes + 1, 4 * no, 128), BF16),
                 pltpu.VMEM((2, 4, npair, tiles(NF), 8, 128), BF16),
                 pltpu.VMEM((2, 4, npair, tiles(ns), 8, 128), BF16),
-                pltpu.VMEM((nd, 4 * no, lanes), BF16),
+                pltpu.VMEM((nd, lanes, 4 * no, 128), BF16),
                 pltpu.VMEM((nd, npair, 4 * no, nv), BF16),
                 pltpu.VMEM((NF, no + 3 * no // 8, 8, 128), F32),
                 pltpu.VMEM((ns, no + 3 * no // 8, 8, 128), F32),
                 pltpu.VMEM((NF, no + 3 * no // 8, 8, 128), F32),
                 pltpu.VMEM((ns, no + 3 * no // 8, 8, 128), F32),
                 dma((2,)), dma((4,)), dma((3,)), dma((2,)), dma((2,)), dma,
-                dma((2,)), dma((NF,)), dma((ns,)),
+                dma((2,)), dma((NF,)), dma((ns,)), pltpu.SemaphoreType.REGULAR,
             ],
             compiler_params=pltpu.CompilerParams(
                 collective_id=0, has_side_effects=True, vmem_limit_bytes=44 * 1024 * 1024),
-        )(a, co.T, cv.T)
+        )(a, *(pltpu.with_memory_space_constraint(t.T, pltpu.HBM) for t in (co, cv)))
         return v1.transpose(0, 2, 1), v2
 
     return jax.shard_map(local_part, mesh=mesh,

time: 50.3 us -> 48.9 us (0.972)
  local copies, waits for them, and re-layouts: 3.61 us -> 2.2 us
    unnamed x6 -> x2, local copies, waits for them, and re-layouts: 3.61 us -> 2.2 us
where the time goes in v6:
time: 48.9 us; the launch traced here: 48.8 us
  Pallas kernels  46 us (94%)
  local copies, waits for them, and re-layouts  2.2 us (4%)
  between operations  0.64 us (1%)
    pallas_call x1, Pallas kernels, local_part(): pl.pallas_call(functools.partial(kernel, np_, n, no, nv), out_shape=(jax....  46 us
    unnamed x2, local copies, waits for them, and re-layouts  2.2 us

profile of v6, /device:TPU:0, one launch (start us, length us, event | category | flops | bytes accessed | tf_op | source)
XLA Modules:
  0.0 48.8 jit_solution(725267798040537523)
XLA Ops:
  0.6 46.0 %shard_map.50 = (f32[88,32,88]{2,1,0:T(8,128)S(1)}, f32[16,88,176]{2,1,0:T(8,128)S(1)}) custom-call(bf16[14,112,112,112]{3,2,1,0:T(8,128)(2,1)} %a_ref.1, bf16[16,112]{1,0:T(8,128)(2,1)} %bitcast.5, bf16[88,112]{1,0:T(8,128)(2,1)} %bitcast.4), custom_call_target="tpu_custom_call" | custom-call | tf_op jit(solution)/shard_map/pallas_call | solution.py:373
  46.6 1.1 %copy.7 = f32[88,88,32]{1,2,0:T(8,128)} copy(f32[88,88,32]{1,2,0:T(8,128)S(1)} %bitcast.3) | data formatting | bytes 1982464
  47.7 1.1 %copy.8 = f32[16,88,176]{2,1,0:T(8,128)} copy(f32[16,88,176]{2,1,0:T(8,128)S(1)} %get-tuple-element.9) | data formatting | bytes 1982464

commit v7 on v6

--- a/solution.py
+++ b/solution.py
@@ -11,6 +11,7 @@
 F32 = jnp.float32
 BF16 = jnp.bfloat16
 NF = 6
+SLOTS = 6
 EXT = 48
 
 
@@ -66,10 +67,8 @@
     KS = [(1, 1, 0), (1, 1, 1), (1, 0, 1), (0, 1, 1), (1, 0, 0), (0, 1, 0), (0, 0, 1), (0, 0, 0)]
     NEAR = [k for k in KS[:-1] if not (k[0] and k[1])]
 
-    def a_copy(p, g):
-        slot = p % 4
-        return pltpu.make_async_copy(a_ref.at[p, pl.ds(16 * g, 16)], a_buf.at[slot, pl.ds(16 * g, 16)],
-                                     a_sem.at[slot])
+    def row_copy(p):
+        return pltpu.make_async_copy(a_ref.at[p], a_buf.at[p % SLOTS], a_sem.at[p % SLOTS])
 
     barrier = pltpu.get_barrier_semaphore()
     for k in NEAR:
@@ -78,8 +77,7 @@
              pltpu.make_async_copy(cvt_hbm, cvt_ref, c_sem.at[1])]
     for cp in coefs:
         cp.start()
-    for g in range(ng):
-        a_copy(0, g).start()
+    row_copy(0).start()
     for cp in coefs:
         cp.wait()
 
@@ -91,8 +89,7 @@
     tile = onehot(iota((n, 8 * n), 0) == iota((n, 8 * n), 1) % n)
     m = dot(rep8, dot(cot, tile).astype(BF16))
     la[...] = jnp.where(iota(m.shape, 0) % 8 == iota(m.shape, 1) // n, m, 0.0).astype(BF16)
-    for g in range(ng):
-        a_copy(1, g).start()
+    row_copy(1).start()
     ww[...] = jnp.zeros_like(ww)
     for par in range(2):
         for j in range(2):
@@ -101,9 +98,8 @@
             sel_o = onehot(iota((no, 256), 1) == iota((no, 256), 0) + 128 + 32 * par + no * j)
             ww[par, 128 * j:128 * j + n, :] = (dot(cv, sel_v) + dot(co, sel_o)).astype(BF16)
 
-    for p in range(2, 4):
-        for g in range(ng):
-            a_copy(p, g).start()
+    for p in range(2, SLOTS):
+        row_copy(p).start()
 
     def span(part, nt):
         return {None: pl.ds(0, tiles(nt)), 0: pl.ds(0, nt), 1: pl.ds(nt, tiles(nt) - nt)}[part]
@@ -163,10 +159,10 @@
     lane_n = iota((n, 128), 1)
 
     def wait_row(p):
-        pltpu.make_async_copy(a_ref.at[p], a_buf.at[p % 4], a_sem.at[p % 4]).wait()
+        row_copy(p).wait()
 
     def steps12(p, par):
-        slot = p % 4
+        slot = p % SLOTS
         for g in range(ng):
             a0 = a_buf[slot, 16 * g:16 * g + 8].reshape(8 * n, n)
             a1 = a_buf[slot, 16 * g + 8:16 * g + 16].reshape(8 * n, n)
@@ -215,13 +211,13 @@
         steps12(2 * i + 1, 1)
         step3(i, (0, 1))
 
-        @pl.when(2 * i + 4 < np_)
+        sends(i)
+
+        @pl.when(2 * i + SLOTS < np_)
         def _():
-            for p in (2 * i + 4, 2 * i + 5):
-                for g in range(ng):
-                    a_copy(p, g).start()
-
-        sends(i)
+            for p in (2 * i + SLOTS, 2 * i + SLOTS + 1):
+                row_copy(p).start()
+
         return 0
 
     wait_row(0)
@@ -236,10 +232,9 @@
     wait_row(1)
     steps12(1, 1)
     step3(0, (1,))
-    for p in (4, 5):
-        for g in range(ng):
-            a_copy(p, g).start()
     sends(0, 1)
+    for p in (SLOTS, SLOTS + 1):
+        row_copy(p).start()
 
     lax.fori_loop(1, npair, pair, 0)
 
@@ -356,6 +351,18 @@
     wait_send(rp.at[pl.ds(0, nd - 1)], s_sem.at[2])
     wait_send(pf, p_sem.at[0])
     wait_send(ps, p_sem.at[1])
+
+
+def out_kernel(v1_ref, v2_ref, o1_ref, o2_ref, sem):
+    cps = []
+    for j, (v, o) in enumerate(((v1_ref, o1_ref), (v2_ref, o2_ref))):
+        m = v.shape[0] // 4
+        for q in range(4):
+            cps.append(pltpu.make_async_copy(v.at[pl.ds(m * q, m)], o.at[pl.ds(m * q, m)], sem.at[4 * j + q]))
+    for cp in cps:
+        cp.start()
+    for cp in cps:
+        cp.wait()
 
 
 def solution(mesh):
@@ -379,7 +386,7 @@
             scratch_shapes=[
                 pltpu.VMEM((no, n), BF16),
                 pltpu.VMEM((nv, n), BF16),
-                pltpu.VMEM((4, n, n, n), BF16),
+                pltpu.VMEM((SLOTS, n, n, n), BF16),
                 pltpu.VMEM((no * 8, n * 8), BF16),
                 pltpu.VMEM((2, 256, 256), BF16),
                 pltpu.VMEM((npair, n, 256), BF16),
@@ -399,12 +406,20 @@
                 pltpu.VMEM((ns, no + 3 * no // 8, 8, 128), F32),
                 pltpu.VMEM((NF, no + 3 * no // 8, 8, 128), F32),
                 pltpu.VMEM((ns, no + 3 * no // 8, 8, 128), F32),
-                dma((2,)), dma((4,)), dma((3,)), dma((2,)), dma((2,)), dma,
+                dma((2,)), dma((SLOTS,)), dma((3,)), dma((2,)), dma((2,)), dma,
                 dma((2,)), dma((NF,)), dma((ns,)), pltpu.SemaphoreType.REGULAR,
             ],
             compiler_params=pltpu.CompilerParams(
-                collective_id=0, has_side_effects=True, vmem_limit_bytes=44 * 1024 * 1024),
+                collective_id=0, has_side_effects=True, vmem_limit_bytes=50 * 1024 * 1024),
         )(a, *(pltpu.with_memory_space_constraint(t.T, pltpu.HBM) for t in (co, cv)))
+        hb = pl.BlockSpec(memory_space=pl.ANY)
+        v1, v2 = pl.pallas_call(
+            out_kernel,
+            out_shape=(jax.ShapeDtypeStruct(v1.shape, F32), jax.ShapeDtypeStruct(v2.shape, F32)),
+            in_specs=[vm, vm], out_specs=(hb, hb),
+            scratch_shapes=[dma((8,))],
+            compiler_params=pltpu.CompilerParams(vmem_limit_bytes=4 * 1024 * 1024),
+        )(v1, v2)
         return v1.transpose(0, 2, 1), v2
 
     return jax.shard_map(local_part, mesh=mesh,

time: 48.9 us -> 48 us (0.982)
  local copies, waits for them, and re-layouts: 2.2 us -> 0 us
  Pallas kernels: 46 us -> 47.2 us
    unnamed x2 -> x0, local copies, waits for them, and re-layouts: 2.2 us -> none
    pallas_call x0 -> x1, Pallas kernels: none -> 1.64 us  [local_part(): pl.pallas_call(out_kernel, out_shape=(jax.ShapeDtypeStruct(v1.shape, F32)...]
where the time goes in v7:
time: 48 us; the launch traced here: 47.9 us
  Pallas kernels  47.2 us (98%)
  between operations  0.64 us (1%)
    pallas_call x1, Pallas kernels, local_part(): pl.pallas_call(functools.partial(kernel, np_, n, no, nv), out_shape=(jax....  45.6 us
    pallas_call x1, Pallas kernels, local_part(): pl.pallas_call(out_kernel, out_shape=(jax.ShapeDtypeStruct(v1.shape, F32)...  1.64 us

profile of v7, /device:TPU:0, one launch (start us, length us, event | category | flops | bytes accessed | tf_op | source)
XLA Modules:
  0.0 47.9 jit_solution(4016312684228200854)
XLA Ops:
  0.6 45.6 %shard_map.50 = (f32[88,32,88]{2,1,0:T(8,128)S(1)}, f32[16,88,176]{2,1,0:T(8,128)S(1)}) custom-call(bf16[14,112,112,112]{3,2,1,0:T(8,128)(2,1)} %a_ref.1, bf16[16,112]{1,0:T(8,128)(2,1)} %bitcast.4, bf16[88,112]{1,0:T(8,128)(2,1)} %bitcast.3), custom_call_target="tpu_custom_call" | custom-call | tf_op jit(solution)/shard_map/pallas_call | solution.py:380
  46.2 1.6 %shard_map.51 = (f32[88,32,88]{2,1,0:T(8,128)}, f32[16,88,176]{2,1,0:T(8,128)}) custom-call(f32[88,32,88]{2,1,0:T(8,128)S(1)} %get-tuple-element.6.v1_ref, f32[16,88,176]{2,1,0:T(8,128)S(1)} %get-tuple-element.7.v2_ref), custom_call_target="tpu_custom_call" | custom-call | tf_op jit(solution)/shard_map/pallas_call | solution.py:416

commit v8 on v7

--- a/solution.py
+++ b/solution.py
@@ -220,15 +220,15 @@
 
         return 0
 
+    sp[...] = jnp.zeros_like(sp)
+    for i in range(npair):
+        cvs[i] = dot(cv, onehot(iota((nv, 256), 1) == iota((nv, 256), 0) + nv * i % 128)).astype(BF16)
     wait_row(0)
     steps12(0, 0)
     step3(0, (0,))
     pl.semaphore_wait(barrier, len(NEAR))
     sends(0, 0)
     pl.semaphore_signal(d_sem, inc=1, device_id=(frag, dest((0, 1, 0))), device_id_type=MESH)
-    sp[...] = jnp.zeros_like(sp)
-    for i in range(npair):
-        cvs[i] = dot(cv, onehot(iota((nv, 256), 1) == iota((nv, 256), 0) + nv * i % 128)).astype(BF16)
     wait_row(1)
     steps12(1, 1)
     step3(0, (1,))
@@ -236,7 +236,18 @@
     for p in (SLOTS, SLOTS + 1):
         row_copy(p).start()
 
-    lax.fori_loop(1, npair, pair, 0)
+    wait_row(2)
+    steps12(2, 0)
+    step3(1, (0,))
+    sends(1, 0)
+    wait_row(3)
+    steps12(3, 1)
+    step3(1, (1,))
+    sends(1, 1)
+    for p in (SLOTS + 2, SLOTS + 3):
+        row_copy(p).start()
+
+    lax.fori_loop(2, npair, pair, 0)
 
     pl.semaphore_wait(d_sem, 1)
     nt = rp.shape[1]

time: 48 us -> 47.7 us (level)
  no operation moved by 1% of the time
where the time goes in v8:
time: 47.7 us; the launch traced here: 47.6 us
  Pallas kernels  46.9 us (98%)
  between operations  0.64 us (1%)
    pallas_call x1, Pallas kernels, local_part(): pl.pallas_call(functools.partial(kernel, np_, n, no, nv), out_shape=(jax....  45.3 us
    pallas_call x1, Pallas kernels, local_part(): pl.pallas_call(out_kernel, out_shape=(jax.ShapeDtypeStruct(v1.shape, F32)...  1.64 us

profile of v8, /device:TPU:0, one launch (start us, length us, event | category | flops | bytes accessed | tf_op | source)
XLA Modules:
  0.0 47.6 jit_solution(6797345569330367315)
XLA Ops:
  0.6 45.3 %shard_map.50 = (f32[88,32,88]{2,1,0:T(8,128)S(1)}, f32[16,88,176]{2,1,0:T(8,128)S(1)}) custom-call(bf16[14,112,112,112]{3,2,1,0:T(8,128)(2,1)} %a_ref.1, bf16[16,112]{1,0:T(8,128)(2,1)} %bitcast.4, bf16[88,112]{1,0:T(8,128)(2,1)} %bitcast.3), custom_call_target="tpu_custom_call" | custom-call | tf_op jit(solution)/shard_map/pallas_call | solution.py:391
  45.9 1.6 %shard_map.51 = (f32[88,32,88]{2,1,0:T(8,128)}, f32[16,88,176]{2,1,0:T(8,128)}) custom-call(f32[88,32,88]{2,1,0:T(8,128)S(1)} %get-tuple-element.6.v1_ref, f32[16,88,176]{2,1,0:T(8,128)S(1)} %get-tuple-element.7.v2_ref), custom_call_target="tpu_custom_call" | custom-call | tf_op jit(solution)/shard_map/pallas_call | solution.py:427
